TPU v7x, 32 devices: a 4x4x1 block of a 4x4x8 slice. The times are simulated.
32 devices in a mesh: dp: 1 (over z), tp: 4 (over y), sp: 8 (over x, core).
Axes of the slice: x: 4, y: 4, z: 1, core: 2. Of those that a mesh axis runs over, the one named last changes fastest.
The devices are a block of a 4x4x8 slice.
Arguments:
- hidden: bfloat16 [32, 4096], P('dp')
- positions: int32 [32], P('dp')
- norm_attn: float32 [4096], replicated
- norm_mlp: float32 [4096], replicated
- w_qkv: bfloat16 [4096, 6144], P(None, 'tp')
- w_out: bfloat16 [4096, 4096], P('tp')
- w_gate_up: bfloat16 [4096, 28672], P(None, 'tp')
- w_down: bfloat16 [14336, 4096], P('tp')
- k_cache: bfloat16 [32, 4096, 8, 128], P('dp', 'sp', 'tp')
- v_cache: bfloat16 [32, 4096, 8, 128], P('dp', 'sp', 'tp')
Outputs:
- output 1: bfloat16 [32, 4096], P('dp')
- output 2: bfloat16 [32, 4096, 8, 128], P('dp', 'sp', 'tp')
- output 3: bfloat16 [32, 4096, 8, 128], P('dp', 'sp', 'tp')
All inputs are finite; a program needn't handle non-finite values.
Results may differ from a plain program's by a relative error of at most 0.00869829.
Values sent between devices are 32-bit elements.
A program may use at most 768 MiB of HBM per device.

v0:
```python
import jax
import jax.numpy as jnp
from jax import lax
from jax.sharding import PartitionSpec as P

WINDOW = 2047
ROPE_BASE = 10000.0
NORM_EPS = 1e-5


def rms_norm(values, gain_vec):
    mean_sq = jnp.mean(values * values, axis=-1, keepdims=True)
    return values * lax.rsqrt(mean_sq + NORM_EPS) * gain_vec


def rope_tables(positions, head_dim):
    inv_freq = ROPE_BASE ** (-jnp.arange(0, head_dim, 2).astype(jnp.float32) / head_dim)
    angles = positions.astype(jnp.float32)[:, None] * inv_freq[None, :]
    angles = jnp.concatenate([angles, angles], axis=-1)
    return jnp.cos(angles), jnp.sin(angles)


def rotate_half(values, cos_tab, sin_tab):
    half_dim = values.shape[-1] // 2
    turned = jnp.concatenate([-values[..., half_dim:], values[..., :half_dim]], axis=-1)
    return values * cos_tab + turned * sin_tab


def new_entries(hidden, positions, norm_attn, w_qkv, kv_count, head_dim):
    num_rows = hidden.shape[0]
    resid_in = hidden.astype(jnp.float32)
    normed = rms_norm(resid_in, norm_attn).astype(jnp.bfloat16)
    group_size = w_qkv.shape[1] // (kv_count * head_dim) - 2
    qkv_proj = jnp.dot(normed, w_qkv, preferred_element_type=jnp.float32).reshape(num_rows, kv_count, group_size + 2, head_dim)
    cos_tab, sin_tab = rope_tables(positions, head_dim)
    q_new = rotate_half(qkv_proj[:, :, :group_size], cos_tab[:, None, None], sin_tab[:, None, None]).astype(jnp.bfloat16)
    k_new = rotate_half(qkv_proj[:, :, group_size], cos_tab[:, None], sin_tab[:, None]).astype(jnp.bfloat16)
    v_new = qkv_proj[:, :, group_size + 1].astype(jnp.bfloat16)
    return resid_in, q_new, k_new, v_new


def write_entry(cache, entry, slot_ids, positions):
    at_slot = (slot_ids[None, :] == positions[:, None])[:, :, None, None]
    return jnp.where(at_slot, entry[:, None], cache)


def window_attention(q_new, k_block, v_block, slot_ids, positions):
    score_scale = q_new.shape[-1] ** -0.5
    scores = jnp.einsum('bkgd,bjkd->bkgj', q_new, k_block, preferred_element_type=jnp.float32) * score_scale
    in_window = (slot_ids[None, :] <= positions[:, None]) & (slot_ids[None, :] >= positions[:, None] - WINDOW)
    scores = jnp.where(in_window[:, None, None, :], scores, -jnp.inf)
    glob_max = lax.pmax(jnp.max(scores, axis=-1), 'sp')
    weights = jnp.exp(scores - glob_max[..., None])
    weight_sum = lax.psum(jnp.sum(weights, axis=-1), 'sp')
    acc_sum = lax.psum(jnp.einsum('bkgj,bjkd->bkgd', weights.astype(jnp.bfloat16), v_block, preferred_element_type=jnp.float32), 'sp')
    return (acc_sum / weight_sum[..., None]).astype(jnp.bfloat16)


def layer_tail(resid_in, attended, norm_mlp, w_out, w_gate_up, w_down):
    out_part = jnp.dot(attended, w_out, preferred_element_type=jnp.float32).astype(jnp.bfloat16).astype(jnp.float32)
    mid_resid = resid_in + lax.psum(out_part, 'tp')
    normed_mlp = rms_norm(mid_resid, norm_mlp).astype(jnp.bfloat16)
    gate_up = jnp.dot(normed_mlp, w_gate_up, preferred_element_type=jnp.float32)
    ffn_local = w_down.shape[0]
    act_vals = (jax.nn.silu(gate_up[:, :ffn_local]) * gate_up[:, ffn_local:]).astype(jnp.bfloat16)
    down_part = jnp.dot(act_vals, w_down, preferred_element_type=jnp.float32).astype(jnp.bfloat16).astype(jnp.float32)
    result = mid_resid + lax.psum(down_part, 'tp')
    return result.astype(jnp.bfloat16)


def solution(mesh):
    cache_spec = P('dp', 'sp', 'tp', None)

    def local_step(hidden, positions, norm_attn, norm_mlp, w_qkv, w_out, w_gate_up, w_down, k_cache, v_cache):
        num_rows, block_len, kv_local, head_dim = k_cache.shape
        resid_in, q_new, k_new, v_new = new_entries(hidden, positions, norm_attn, w_qkv, kv_local, head_dim)
        slot_ids = lax.axis_index('sp') * block_len + jnp.arange(block_len)
        k_upd = write_entry(k_cache, k_new, slot_ids, positions)
        v_upd = write_entry(v_cache, v_new, slot_ids, positions)
        attended = window_attention(q_new, k_upd, v_upd, slot_ids, positions).reshape(num_rows, -1)
        result = layer_tail(resid_in, attended, norm_mlp, w_out, w_gate_up, w_down)
        return result, k_upd, v_upd

    return jax.shard_map(local_step, mesh=mesh, in_specs=(P('dp', None), P('dp'), P(None), P(None), P(None, 'tp'), P('tp', None), P(None, 'tp'), P('tp', None), cache_spec, cache_spec), out_specs=(P('dp', None), cache_spec, cache_spec), check_vma=False)
```

profile of v0, /device:TPU:97, one launch (start us, length us, event | category | flops | bytes accessed | tf_op | source)
XLA Modules:
  0.0 260.2 jit_solution(4891797256271544712)
XLA Ops:
  7.2 0.1 all-reduce.4.cloned.1.call-start
  7.3 1.1 fusion.12
  8.4 0.0 copy-start.4
  8.4 7.0 %fusion.20 = f32[32,1536]{1,0:T(8,128)S(1)} fusion(bf16[4096,1536]{1,0:T(8,128)(2,1)} %param.14, bf16[32,4096]{1,0:T(8,128)(2,1)} %param.10, f32[4096]{0:T(1024)} %param.12, f32[32]{0:T(128)S(1)} %add_rsqrt_fusion.1), kind=kOutput, calls=%fused_computation.27 | convolution fusion | flops 403177472 | bytes 13058176 | tf_op jit(solution)/shard_map/dot_general | solution.py:34
  15.4 0.1 reshape.247
  15.6 0.1 slice_negate_fusion
  15.7 0.0 copy-done.4
  15.7 0.1 broadcast_multiply_fusion
  15.8 0.1 fusion.37
  16.0 0.1 slice_negate_fusion.1
  16.1 0.1 compare_and_fusion
  16.2 0.1 fusion.35
  16.3 26.2 %broadcast_select_fusion.1 = (bf16[32,512,2,128]{3,2,1,0:T(2,128)(2,1)S(1)}, bf16[32,512,2,128]{3,2,1,0:T(2,128)(2,1)}) fusion(bf16[32,512,2,128]{3,2,1,0:T(2,128)(2,1)} %param.18, pred[32,512]{1,0:T(8,128)(4,1)S(1)} %get-tuple-element.12, bf16[32,2,128]{2,1,0:T(2,128)(2,1)S(1)} %fusion.35, bf16[32,512,2,128]{3,2,1,0:T(2,128)(2,1)} %param.19, ...), kind=kLoop, calls=%fused_computation.1 | loop fusion | flops 8388608 | bytes 33603584 | tf_op jit(solution)/shard_map/jit(_where)/select_n | solution.py:44
  42.5 0.0 copy-start
  42.5 3.4 %copy-done = bf16[32,512,2,128]{3,2,1,0:T(2,128)(2,1)} copy-done((bf16[32,512,2,128]{3,2,1,0:T(2,128)(2,1)}, bf16[32,512,2,128]{3,2,1,0:T(2,128)(2,1)S(1)}, u32[]{:S(2)}) %copy-start) | copy-done | bytes 8388632
  45.9 2.4 fusion.40
  48.3 24.0 %pmax.7 = f32[32,2,4]{2,1,0:T(2,128)S(1)} all-reduce(f32[32,2,4]{2,1,0:T(2,128)S(1)} %get-tuple-element.15), channel_id=1, replica_groups=mesh['dp'=1,'tp'=4,'sp'=8] {'sp'}, use_global_device_ids=true, to_apply=%region_2.3 | all-reduce | flops 256 | bytes 2048 | tf_op jit(solution)/shard_map/pmax | solution.py:52
  72.4 5.3 %fusion = f32[32,2,4,128]{3,2,1,0:T(4,128)} fusion(bf16[32,512,2,128]{3,2,1,0:T(2,128)(2,1)} %get-tuple-element.8, f32[32,2,4,512]{3,2,1,0:T(4,128)S(1)} %get-tuple-element.16, f32[32,2,4]{2,1,0:T(2,128)S(1)} %pmax.7), kind=kOutput, calls=%fused_computation.2 | convolution fusion | flops 33816576 | bytes 9044992 | tf_op jit(solution)/shard_map/bkgj,bjkd->bkgd/dot_general | solution.py:55
  77.6 0.1 all-reduce.4.cloned.1.call-update
  77.7 0.0 copy-start.1
  77.7 0.1 all-reduce.6.cloned.1.call-start
  77.8 0.4 fusion.16
  78.2 23.7 %psum.29 = f32[32,2,4]{2,1,0:T(2,128)S(1)} all-reduce(f32[32,2,4]{2,1,0:T(2,128)S(1)} %fusion.16), channel_id=1, replica_groups=mesh['dp'=1,'tp'=4,'sp'=8] {'sp'}, use_global_device_ids=true, to_apply=%region_5.6 | all-reduce | flops 256 | bytes 2048 | tf_op jit(solution)/shard_map/psum | solution.py:54
  101.8 31.8 %all-reduce.4.cloned.1.call-done = f32[32,2,4,128]{3,2,1,0:T(4,128)} async-done(((f32[32,2,4,128]{3,2,1,0:T(4,128)}), f32[32,2,4,128]{3,2,1,0:T(4,128)}) %all-reduce.4.cloned.1.call-update) | async-done | bytes 131088 | tf_op jit(solution)/shard_map/psum | solution.py:55
  133.6 1.0 divide_convert_fusion
  134.7 0.0 copy-start.3
  134.7 5.7 %fusion.5 = f32[32,4096]{1,0:T(8,128)} fusion(bf16[32,1024]{1,0:T(8,128)(2,1)S(1)} %reshape.248, bf16[1024,4096]{1,0:T(8,128)(2,1)} %param.15), kind=kOutput, calls=%fused_computation.9 | convolution fusion | flops 268697600 | bytes 8978432 | tf_op jit(solution)/shard_map/dot_general | solution.py:60
  140.5 0.1 all-reduce.6.cloned.1.call-update
  140.5 0.2 all-reduce.8.cloned.1.call-start
  140.8 36.8 %all-reduce.6.cloned.1.call-done = f32[32,4096]{1,0:T(8,128)} async-done(((f32[32,4096]{1,0:T(8,128)}), f32[32,4096]{1,0:T(8,128)}) %all-reduce.6.cloned.1.call-update) | async-done | bytes 524304 | tf_op jit(solution)/shard_map/psum | solution.py:61
  177.6 0.0 copy-done.1
  177.6 1.2 multiply_reduce_fusion
  178.8 0.0 copy-done.3
  178.8 21.6 %fusion.19 = f32[32,7168]{1,0:T(8,128)S(1)} fusion(bf16[4096,7168]{1,0:T(8,128)(2,1)} %param.16, f32[4096]{0:T(1024)S(1)} %copy-done.3, f32[32]{0:T(128)S(1)} %add_rsqrt_fusion, f32[32,4096]{1,0:T(8,128)} %all-reduce.6.cloned.1.call-done, bf16[32,4096]{1,0:T(8,128)(2,1)S(1)} %copy-done.1), kind=kOutput, calls=%fused_computation.26 | convolution fusion | flops 1879703552 | bytes 60440704 | tf_op jit(solution)/shard_map/dot_general | solution.py:63
  200.4 0.0 copy-start.2
  200.4 12.9 %fusion.4 = f32[32,4096]{1,0:T(8,128)} fusion(bf16[3584,4096]{1,0:T(8,128)(2,1)} %param.17, f32[32,7168]{1,0:T(8,128)S(1)} %fusion.19), kind=kOutput, calls=%fused_computation.7 | convolution fusion | flops 940474368 | bytes 30801920 | tf_op jit(solution)/shard_map/dot_general | solution.py:66
  213.3 0.1 all-reduce.8.cloned.1.call-update
  213.4 38.4 %all-reduce.8.cloned.1.call-done = f32[32,4096]{1,0:T(8,128)} async-done(((f32[32,4096]{1,0:T(8,128)}), f32[32,4096]{1,0:T(8,128)}) %all-reduce.8.cloned.1.call-update) | async-done | bytes 524304 | tf_op jit(solution)/shard_map/psum | solution.py:67
  251.8 0.0 copy-done.2
  251.8 1.8 add_convert_fusion
  (10 shorter events, 0.2 us)
Async XLA Ops:
  7.2 126.5 %all-reduce.4.cloned.1.call-start = ((), (), s32[]{:S(2)}) async-start(), calls=%async_computation | async-start | bytes 262144 | tf_op jit(solution)/shard_map/psum | solution.py:55
  8.4 7.3 %copy-start.4 = (s32[32]{0:T(128)S(1)}, s32[32]{0:T(128)}, u32[]{:S(2)}) copy-start(s32[32]{0:T(128)} %param.11) | copy-start | bytes 388
  42.5 3.4 %copy-start = (bf16[32,512,2,128]{3,2,1,0:T(2,128)(2,1)}, bf16[32,512,2,128]{3,2,1,0:T(2,128)(2,1)S(1)}, u32[]{:S(2)}) copy-start(bf16[32,512,2,128]{3,2,1,0:T(2,128)(2,1)S(1)} %get-tuple-element.7) | copy-start | bytes 25165828
  77.7 99.9 %copy-start.1 = (bf16[32,4096]{1,0:T(8,128)(2,1)S(1)}, bf16[32,4096]{1,0:T(8,128)(2,1)}, u32[]{:S(2)}) copy-start(bf16[32,4096]{1,0:T(8,128)(2,1)} %param.10) | copy-start | bytes 786436
  77.7 99.9 %all-reduce.6.cloned.1.call-start = ((), (), s32[]{:S(2)}) async-start(), calls=%async_computation.1 | async-start | bytes 1048576 | tf_op jit(solution)/shard_map/psum | solution.py:61
  134.7 44.1 %copy-start.3 = (f32[4096]{0:T(1024)S(1)}, f32[4096]{0:T(1024)}, u32[]{:S(2)}) copy-start(f32[4096]{0:T(1024)} %param.13) | copy-start | bytes 49156
  140.5 111.3 %all-reduce.8.cloned.1.call-start = ((), (), s32[]{:S(2)}) async-start(), calls=%async_computation.2 | async-start | bytes 1048576 | tf_op jit(solution)/shard_map/psum | solution.py:67
  200.4 51.4 %copy-start.2 = (f32[32,4096]{1,0:T(8,128)S(1)}, f32[32,4096]{1,0:T(8,128)}, u32[]{:S(2)}) copy-start(f32[32,4096]{1,0:T(8,128)} %all-reduce.6.cloned.1.call-done) | copy-start | bytes 1572868
Sparse Core Ops, SparseCore 0:
  77.8 55.7 all-reduce.3
  140.7 36.8 all-reduce.5
  213.5 38.2 all-reduce.7
where the time goes:
time: 262 us; the launch traced here: 260 us
  waiting for transfers between devices  107 us (41%)
  matrix products  55 us (21%)
  blocking collectives  47.7 us (18%)
  other arithmetic  32.4 us (12%)
  between operations  14 us (5%)
  local copies, waits for them, and re-layouts  3.6 us (1%)
    psum x1, waiting for transfers between devices, layer_tail(): result = mid_resid + lax.psum(down_part, 'tp')  38.4 us
    psum x1, waiting for transfers between devices, layer_tail(): mid_resid = resid_in + lax.psum(out_part, 'tp')  36.8 us
    psum x1, waiting for transfers between devices, window_attention(): lax.psum(jnp.einsum('bkgj,bjkd->bkgd', weights.astype(jnp.bfloat16), v_bl...  31.8 us
    select_n x1, other arithmetic, write_entry(): return jnp.where(at_slot, entry[:, None], cache)  26.2 us
    pmax x1, blocking collectives, window_attention(): glob_max = lax.pmax(jnp.max(scores, axis=-1), 'sp')  24 us
    psum x1, blocking collectives, window_attention(): weight_sum = lax.psum(jnp.sum(weights, axis=-1), 'sp')  23.7 us
    dot_general x1, matrix products, layer_tail(): gate_up = jnp.dot(normed_mlp, w_gate_up, preferred_element_type=jnp.float32)  21.6 us
    dot_general x1, matrix products, layer_tail(): jnp.dot(act_vals, w_down, preferred_element_type=jnp.float32)  12.9 us
  transfers between devices with their start and end apart: 3, of which 3 were waited for; matrix products, arithmetic and copies ran while one was open for 0% of the time, Pallas kernels for 0%

commit v1 on v0

v1 whole, which is shorter than its diff:
```python
import functools

import jax
import jax.numpy as jnp
import numpy as np
from jax import lax
from jax.experimental import pallas as pl
from jax.experimental.pallas import tpu as pltpu
from jax.sharding import PartitionSpec as P

WINDOW = 2047
ROPE_BASE = 10000.0
NORM_EPS = 1e-5
MESH = pl.DeviceIdType.MESH
LANES = 128
QKV_CHUNKS = 4
VMEM_LIMIT = 60 * 1024 * 1024
F32, BF16 = jnp.float32, jnp.bfloat16


def dot(lhs, rhs):
    return jnp.dot(lhs, rhs, preferred_element_type=F32)


def dot_t(lhs, rhs):
    return lax.dot_general(lhs, rhs, (((1,), (1,)), ((), ())), preferred_element_type=F32)


def round_bf16(values):
    return values.astype(BF16).astype(F32)


def row_scale(values):
    return lax.rsqrt(jnp.mean(values * values, axis=-1, keepdims=True) + NORM_EPS)


def attend_kernel(dims, pos_ref, hid_ref, gain_ref, freq_ref, w_hbm, k_hbm, v_hbm, ko_hbm, vo_hbm, part_ref, resid_ref,
                  w_buf, k_buf, v_buf, norm_buf, proj_buf, q_buf, new_buf, w_sem, k_sem, v_sem, ko_sem, vo_sem):
    rows, block_len, kv_count, group, shares = dims
    heads = kv_count * group
    per_share = rows // shares
    w_rows = w_buf.shape[0] // QKV_CHUNKS

    def w_copy(c):
        part = pl.ds(c * w_rows, w_rows)
        return pltpu.make_async_copy(w_hbm.at[part], w_buf.at[part], w_sem.at[c])

    def cache_copy(src, dst, sem, g):
        part = pl.ds(g * per_share, per_share)
        return pltpu.make_async_copy(src.at[part], dst.at[part], sem.at[g])

    for c in range(QKV_CHUNKS):
        w_copy(c).start()
    for g in range(shares):
        cache_copy(k_hbm, k_buf, k_sem, g).start()
        cache_copy(v_hbm, v_buf, v_sem, g).start()

    resid = hid_ref[...].astype(F32)
    for s in range(shares):
        resid_ref[s] = resid[s * per_share:(s + 1) * per_share]
    norm_buf[...] = (resid * row_scale(resid) * gain_ref[...]).astype(BF16)

    row_id = lax.broadcasted_iota(jnp.int32, (8, LANES), 0)
    tiles = []
    for r in range(rows // 8):
        tile = jnp.zeros((8, LANES), jnp.int32)
        for i in range(8):
            tile = jnp.where(row_id == i, pos_ref[r * 8 + i], tile)
        tiles.append(tile)
    angles = jnp.concatenate(tiles, axis=0).astype(F32) * freq_ref[...]
    cos_tab = jnp.cos(angles)
    sin_tab = jnp.sin(angles)
    lane_id = lax.broadcasted_iota(jnp.int32, (rows, LANES), 1)
    sin_tab = jnp.where(lane_id < LANES // 2, -sin_tab, sin_tab)

    def rope(values):
        return values * cos_tab + pltpu.roll(values, LANES // 2, axis=1) * sin_tab

    for c in range(QKV_CHUNKS):
        part = slice(c * w_rows, (c + 1) * w_rows)
        w_copy(c).wait()
        term = dot(norm_buf[:, part], w_buf[part, :])
        proj_buf[...] = term if c == 0 else proj_buf[...] + term

    for kv in range(kv_count):
        base = kv * (group + 2) * LANES
        for g in range(group):
            q_new = round_bf16(rope(proj_buf[:, base + g * LANES:base + (g + 1) * LANES]))
            q_buf[pl.ds(kv * group + g, rows, stride=heads), :] = q_new
        k_col = base + group * LANES
        new_buf[pl.ds(kv, rows, stride=8), :] = round_bf16(rope(proj_buf[:, k_col:k_col + LANES]))
        new_buf[pl.ds(kv_count + kv, rows, stride=8), :] = round_bf16(proj_buf[:, k_col + LANES:k_col + 2 * LANES])

    start = lax.axis_index('sp') * block_len
    score_scale = LANES ** -0.5
    tile_rows = 8 * kv_count
    tile_id = lax.broadcasted_iota(jnp.int32, (tile_rows, LANES), 0)
    col_id = lax.broadcasted_iota(jnp.int32, (heads, block_len * kv_count), 1)
    head_id = lax.broadcasted_iota(jnp.int32, (heads, block_len * kv_count), 0)
    own_kv = lax.rem(col_id, kv_count) == head_id // group
    slot_id = jnp.where(own_kv, start + col_id // kv_count, -1)
    stat_lane = lax.broadcasted_iota(jnp.int32, (heads, LANES), 1)

    def write_row(buf, b, slot, first):
        base = pl.multiple_of((slot // 8) * tile_rows, tile_rows)
        tile = buf[b, pl.ds(base, tile_rows), :].astype(F32)
        lines = new_buf[pl.ds(pl.multiple_of(b * 8, 8), 8), :]
        new = jnp.zeros((tile_rows, LANES), F32)
        for kv in range(kv_count):
            line = lines[first + kv:first + kv + 1, :]
            new = jnp.where(lax.rem(tile_id, kv_count) == kv, line, new)
        hit = tile_id // kv_count == lax.rem(slot, 8)
        buf[b, pl.ds(base, tile_rows), :] = jnp.where(hit, new, tile).astype(BF16)

    def share_step(g, carry):
        cache_copy(k_hbm, k_buf, k_sem, g).wait()
        cache_copy(v_hbm, v_buf, v_sem, g).wait()
        for i in range(per_share):
            b = g * per_share + i
            slot = pos_ref[b] - start

            @pl.when(jnp.logical_and(slot >= 0, slot < block_len))
            def _():
                write_row(k_buf, b, slot, 0)
                write_row(v_buf, b, slot, kv_count)

        cache_copy(k_buf, ko_hbm, ko_sem, g).start()
        cache_copy(v_buf, vo_hbm, vo_sem, g).start()
        stats = jnp.zeros((heads, LANES), F32)
        for i in range(per_share):
            b = g * per_share + i
            pos = pos_ref[b]
            q_rows = q_buf[pl.ds(pl.multiple_of(b * heads, heads), heads), :].astype(BF16)
            scores = dot_t(q_rows, k_buf[b]) * score_scale
            seen = (slot_id <= pos) & (slot_id >= jnp.maximum(pos - WINDOW, 0))
            scores = jnp.where(seen, scores, -jnp.inf)
            top = jnp.max(scores, axis=-1, keepdims=True)
            base = jnp.where(top == -jnp.inf, 0.0, top)
            weights = jnp.exp(scores - base)
            total = jnp.sum(weights, axis=-1, keepdims=True)
            part_ref[g, i] = dot(weights.astype(BF16), v_buf[b])
            stats = jnp.where(stat_lane == i, top, stats)
            stats = jnp.where(stat_lane == per_share + i, total, stats)
        part_ref[g, per_share] = stats
        return carry

    lax.fori_loop(0, shares, share_step, 0)
    for g in range(shares):
        cache_copy(k_buf, ko_hbm, ko_sem, g).wait()
        cache_copy(v_buf, vo_hbm, vo_sem, g).wait()


def tail_kernel(n_tp, n_sp, part_ref, resid_hbm, gain_ref, wo_hbm, wgu_hbm, wd_hbm, out_ref,
                wo_buf, wg_buf, wu_buf, wd_buf, resid_buf, part_in, att_buf, y1_buf, x1_in, x1_buf, r2_buf,
                a_out, a_in, y2_buf, x2_in, w_sem, b_send, b_recv, y1_send, y1_recv, g1_send, g1_recv,
                a_send, a_recv, y2_send, y2_recv, g2_send, g2_recv):
    t = lax.axis_index('tp')
    s = lax.axis_index('sp')
    chip, core = s // 2, lax.rem(s, 2)
    n_chip = n_sp // 2
    mate = chip * 2 + 1 - core
    units = wd_hbm.shape[0]
    chip_tiles = units // LANES // n_chip
    core_tiles = (chip_tiles + 1) // 2
    width = core_tiles * LANES
    model = wo_hbm.shape[1]
    half = model // 2
    col = pl.multiple_of((chip * chip_tiles + core * (chip_tiles - core_tiles)) * LANES, LANES)
    loads = [
        pltpu.make_async_copy(resid_hbm.at[s], resid_buf, w_sem.at[0]),
        pltpu.make_async_copy(wo_hbm, wo_buf, w_sem.at[1]),
        pltpu.make_async_copy(wgu_hbm.at[:, pl.ds(col, width)], wg_buf, w_sem.at[2]),
        pltpu.make_async_copy(wgu_hbm.at[:, pl.ds(pl.multiple_of(units + col, LANES), width)], wu_buf, w_sem.at[3]),
        pltpu.make_async_copy(wd_hbm.at[:, pl.ds(pl.multiple_of(core * half, half), half)], wd_buf, w_sem.at[4]),
    ]
    for load in loads:
        load.start()

    def sp_at(k):
        return lax.rem(s + k, n_sp)

    def sp_from(k):
        return lax.rem(s + n_sp - k, n_sp)

    def tp_at(k):
        return lax.rem(t + k, n_tp)

    def tp_from(k):
        return lax.rem(t + n_tp - k, n_tp)

    barrier = pltpu.get_barrier_semaphore()
    for k in range(1, n_sp):
        pl.semaphore_signal(barrier, inc=1, device_id={'sp': sp_at(k)}, device_id_type=MESH)
    for k in range(1, n_tp):
        pl.semaphore_signal(barrier, inc=1, device_id={'tp': tp_at(k)}, device_id_type=MESH)
    pl.semaphore_wait(barrier, n_sp + n_tp - 2)

    def remote(src, dst, send, recv, device):
        return pltpu.make_async_remote_copy(src_ref=src, dst_ref=dst, send_sem=send, recv_sem=recv,
                                            device_id=device, device_id_type=MESH)

    def exchange_sp(src_of, buf, send, recv):
        copies = [remote(src_of(sp_at(k)), buf.at[s], send.at[k - 1], recv.at[k - 1], {'sp': sp_at(k)}) for k in range(1, n_sp)]
        for copy in copies:
            copy.start()

        def finish():
            for k in range(1, n_sp):
                remote(buf.at[s], buf.at[sp_from(k)], send.at[k - 1], recv.at[k - 1], {'sp': sp_at(k)}).wait_recv()
            for copy in copies:
                copy.wait_send()
        return finish

    def exchange_tp(buf, send, recv):
        copies = [remote(buf.at[t], buf.at[t], send.at[k - 1], recv.at[k - 1], {'tp': tp_at(k)}) for k in range(1, n_tp)]
        for copy in copies:
            copy.start()
        for k in range(1, n_tp):
            remote(buf.at[t], buf.at[tp_from(k)], send.at[k - 1], recv.at[k - 1], {'tp': tp_at(k)}).wait_recv()
        for copy in copies:
            copy.wait_send()

    def gather_sp(buf, send, recv):
        def far(k):
            return lax.rem(chip + k, n_chip) * 2 + core

        def far_from(k, c):
            return lax.rem(chip + n_chip - k, n_chip) * 2 + c
        copies = [remote(buf.at[s], buf.at[s], send.at[k], recv.at[k], {'sp': far(k)}) for k in range(1, n_chip)]
        copies.append(remote(buf.at[s], buf.at[s], send.at[0], recv.at[0], {'sp': mate}))
        for copy in copies:
            copy.start()
        for k in sorted(range(1, n_chip), key=lambda k: min(k, n_chip - k)):
            slot = far_from(k, core)
            remote(buf.at[s], buf.at[slot], send.at[k], recv.at[k], {'sp': far(k)}).wait_recv()
            relay = remote(buf.at[slot], buf.at[slot], send.at[n_chip + k - 1], recv.at[n_chip + k - 1], {'sp': mate})
            relay.start()
            copies.append(relay)
        remote(buf.at[s], buf.at[mate], send.at[0], recv.at[0], {'sp': mate}).wait_recv()
        for k in range(1, n_chip):
            slot = far_from(k, 1 - core)
            remote(buf.at[s], buf.at[slot], send.at[n_chip + k - 1], recv.at[n_chip + k - 1], {'sp': mate}).wait_recv()
        for copy in copies:
            copy.wait_send()

    per_share = part_ref.shape[1] - 1
    heads = part_ref.shape[2]
    finish = exchange_sp(lambda peer: part_ref.at[peer], part_in, b_send, b_recv)
    part_in[s] = part_ref[s]
    finish()
    stats = [part_in[j, per_share] for j in range(n_sp)]
    top = functools.reduce(jnp.maximum, stats)
    scales = [jnp.exp(st - top) for st in stats]
    total = sum(sc * pltpu.roll(st, LANES - per_share, axis=1) for sc, st in zip(scales, stats))
    for i in range(per_share):
        acc = sum(part_in[j, i] * scales[j][:, i:i + 1] for j in range(n_sp))
        att_buf[i * heads:(i + 1) * heads, :] = round_bf16(acc / total[:, i:i + 1])
    attended = jnp.concatenate([att_buf[pl.ds(h, per_share, stride=heads), :] for h in range(heads)], axis=1).astype(BF16)

    loads[0].wait()
    loads[1].wait()
    y1_buf[t] = round_bf16(dot(attended, wo_buf[...]))
    exchange_tp(y1_buf, y1_send, y1_recv)
    out_sum = functools.reduce(jnp.add, [y1_buf[j] for j in range(n_tp)])
    x1_in[s] = resid_buf[...] + out_sum
    gather_sp(x1_in, g1_send, g1_recv)

    rows = n_sp * per_share
    for j in range(n_sp):
        x1_buf[j * per_share:(j + 1) * per_share, :] = x1_in[j]
    chunk = 4 * LANES
    square = jnp.zeros((rows, LANES), F32)
    for c in range(model // LANES):
        piece = x1_buf[:, c * LANES:(c + 1) * LANES]
        square = square + piece * piece
    scale = lax.rsqrt(jnp.sum(square, axis=-1, keepdims=True) / model + NORM_EPS)
    for c in range(model // chunk):
        part = slice(c * chunk, (c + 1) * chunk)
        r2_buf[:, part] = (x1_buf[:, part] * scale * gain_ref[:, part]).astype(BF16)

    loads[2].wait()
    gate = dot(r2_buf[...], wg_buf[...])
    loads[3].wait()
    up = dot(r2_buf[...], wu_buf[...])
    act = round_bf16(gate * jax.nn.sigmoid(gate) * up)
    chip_rows = 2 * per_share
    for j in range(n_chip):
        a_out[j] = act[j * chip_rows:(j + 1) * chip_rows]
    finish = exchange_sp(lambda peer: a_out.at[peer // 2], a_in, a_send, a_recv)
    a_in[s] = a_out[chip]
    finish()
    pieces = []
    for j in range(n_chip):
        pieces.append(a_in[2 * j])
        pieces.append(a_in[2 * j + 1][:, (2 * core_tiles - chip_tiles) * LANES:])
    act_rows = jnp.concatenate(pieces, axis=1).astype(BF16)

    loads[4].wait()
    y2_buf[t] = round_bf16(dot(act_rows, wd_buf[...]))
    exchange_tp(y2_buf, y2_send, y2_recv)
    down_sum = functools.reduce(jnp.add, [y2_buf[j] for j in range(n_tp)])
    own = x1_buf[pl.ds(pl.multiple_of(chip * chip_rows, chip_rows), chip_rows), pl.ds(pl.multiple_of(core * half, half), half)]
    x2_in[s] = own + down_sum
    gather_sp(x2_in, g2_send, g2_recv)
    for j in range(0, n_chip, 2):
        for c in range(2):
            pair = jnp.concatenate([x2_in[2 * j + c], x2_in[2 * j + 2 + c]], axis=0)
            out_ref[j * chip_rows:(j + 2) * chip_rows, c * half:(c + 1) * half] = pair.astype(BF16)


def vmem():
    return pl.BlockSpec(memory_space=pltpu.VMEM)


def hbm():
    return pl.BlockSpec(memory_space=pl.ANY)


def solution(mesh):
    n_tp, n_sp = mesh.shape['tp'], mesh.shape['sp']
    cache_spec = P('dp', 'sp', 'tp', None)

    def local_step(hidden, positions, norm_attn, norm_mlp, w_qkv, w_out, w_gate_up, w_down, k_cache, v_cache):
        rows, block_len, kv_count, head_dim = k_cache.shape
        model = hidden.shape[1]
        group = w_qkv.shape[1] // (kv_count * head_dim) - 2
        heads = kv_count * group
        shares = n_sp
        per_share = rows // shares
        flat = (rows, block_len * kv_count, head_dim)
        inv_freq = ROPE_BASE ** (-np.arange(0, head_dim, 2) / head_dim)
        freq = jnp.asarray(np.concatenate([inv_freq, inv_freq])[None, :], F32)
        dma = pltpu.SemaphoreType.DMA

        k_upd, v_upd, parts, resid = pl.pallas_call(
            functools.partial(attend_kernel, (rows, block_len, kv_count, group, shares)),
            out_shape=(
                jax.ShapeDtypeStruct(flat, BF16),
                jax.ShapeDtypeStruct(flat, BF16),
                jax.ShapeDtypeStruct((shares, per_share + 1, heads, head_dim), F32),
                jax.ShapeDtypeStruct((shares, per_share, model), F32),
            ),
            in_specs=[pl.BlockSpec(memory_space=pltpu.SMEM), vmem(), vmem(), vmem(), hbm(), hbm(), hbm()],
            out_specs=(hbm(), hbm(), vmem(), vmem()),
            scratch_shapes=[
                pltpu.VMEM(w_qkv.shape, BF16),
                pltpu.VMEM(flat, BF16),
                pltpu.VMEM(flat, BF16),
                pltpu.VMEM((rows, model), BF16),
                pltpu.VMEM((rows, w_qkv.shape[1]), F32),
                pltpu.VMEM((rows * heads, head_dim), F32),
                pltpu.VMEM((rows * 8, head_dim), F32),
                dma((QKV_CHUNKS,)), dma((shares,)), dma((shares,)), dma((shares,)), dma((shares,)),
            ],
            compiler_params=pltpu.CompilerParams(vmem_limit_bytes=VMEM_LIMIT),
            name='attend',
        )(positions, hidden, norm_attn[None, :], freq, w_qkv, k_cache.reshape(flat), v_cache.reshape(flat))

        units = w_down.shape[0]
        n_chip = n_sp // 2
        chip_tiles = units // LANES // n_chip
        width = (chip_tiles + 1) // 2 * LANES
        chip_rows = 2 * per_share
        half = model // 2
        result = pl.pallas_call(
            functools.partial(tail_kernel, n_tp, n_sp),
            out_shape=jax.ShapeDtypeStruct((rows, model), BF16),
            in_specs=[vmem(), hbm(), vmem(), hbm(), hbm(), hbm()],
            out_specs=vmem(),
            scratch_shapes=[
                pltpu.VMEM(w_out.shape, BF16),
                pltpu.VMEM((model, width), BF16),
                pltpu.VMEM((model, width), BF16),
                pltpu.VMEM((units, half), BF16),
                pltpu.VMEM((per_share, model), F32),
                pltpu.VMEM((n_sp, per_share + 1, heads, head_dim), F32),
                pltpu.VMEM((per_share * heads, head_dim), F32),
                pltpu.VMEM((n_tp, per_share, model), F32),
                pltpu.VMEM((n_sp, per_share, model), F32),
                pltpu.VMEM((rows, model), F32),
                pltpu.VMEM((rows, model), BF16),
                pltpu.VMEM((n_chip, chip_rows, width), F32),
                pltpu.VMEM((n_sp, chip_rows, width), F32),
                pltpu.VMEM((n_tp, chip_rows, half), F32),
                pltpu.VMEM((n_sp, chip_rows, half), F32),
                dma((5,)),
                dma((n_sp - 1,)), dma((n_sp - 1,)),
                dma((n_tp - 1,)), dma((n_tp - 1,)),
                dma((n_sp - 1,)), dma((n_sp - 1,)),
                dma((n_sp - 1,)), dma((n_sp - 1,)),
                dma((n_tp - 1,)), dma((n_tp - 1,)),
                dma((n_sp - 1,)), dma((n_sp - 1,)),
            ],
            compiler_params=pltpu.CompilerParams(vmem_limit_bytes=VMEM_LIMIT, collective_id=0, has_side_effects=True),
            name='tail',
        )(parts, resid, norm_mlp[None, :], w_out, w_gate_up, w_down)
        return result, k_upd.reshape(k_cache.shape), v_upd.reshape(v_cache.shape)

    return jax.shard_map(local_step, mesh=mesh, in_specs=(P('dp', None), P('dp'), P(None), P(None), P(None, 'tp'), P('tp', None), P(None, 'tp'), P('tp', None), cache_spec, cache_spec), out_specs=(P('dp', None), cache_spec, cache_spec), check_vma=False)
```

time: 262 us -> 71.4 us (0.27)
  waiting for transfers between devices: 107 us -> 0 us
  Pallas kernels: 0 us -> 68.9 us
  matrix products: 55 us -> 0 us
  blocking collectives: 47.7 us -> 0 us
  other arithmetic: 32.4 us -> 0 us
  between operations: 14 us -> 0.65 us
    psum x3 -> x0, waiting for transfers between devices: 107 us -> none  [the longest x1 38.4 us: layer_tail(): result = mid_resid + lax.psum(down_part, 'tp')]
    pallas_call x0 -> x2, Pallas kernels: none -> 68.9 us  [the longest x1 46.2 us: local_step(): pl.pallas_call(functools.partial(tail_kernel, n_tp, n_sp), out_shape=jax....]
    dot_general x6 -> x0, matrix products: 55 us -> none  [the longest x1 21.6 us: layer_tail(): gate_up = jnp.dot(normed_mlp, w_gate_up, preferred_element_type=jnp.float32)]
    select_n x1 -> x0, other arithmetic: 26.2 us -> none  [write_entry(): return jnp.where(at_slot, entry[:, None], cache)]
    pmax x1 -> x0, blocking collectives: 24 us -> none  [window_attention(): glob_max = lax.pmax(jnp.max(scores, axis=-1), 'sp')]
    psum x1 -> x0, blocking collectives: 23.7 us -> none  [window_attention(): weight_sum = lax.psum(jnp.sum(weights, axis=-1), 'sp')]
    convert_element_type x3 -> x0, other arithmetic: 2.96 us -> none  [the longest x1 1.81 us: layer_tail(): return result.astype(jnp.bfloat16)]
    reduce_sum x3 -> x0, other arithmetic: 2.69 us -> none  [the longest x2 2.33 us: rms_norm(): mean_sq = jnp.mean(values * values, axis=-1, keepdims=True)]
  transfers between devices with their start and end apart: 3 -> 0, of which waited for: 3 -> 0; matrix products, arithmetic and copies ran while one was open for 0% -> 0% of each run, Pallas kernels for 0% -> 0%
where the time goes in v1:
time: 71.4 us; the launch traced here: 71.2 us
  Pallas kernels  68.9 us (96%)
  local copies, waits for them, and re-layouts  1.67 us (2%)
    pallas_call x1, Pallas kernels, local_step(): pl.pallas_call(functools.partial(tail_kernel, n_tp, n_sp), out_shape=jax....  46.2 us
    pallas_call x1, Pallas kernels, local_step(): pl.pallas_call(functools.partial(attend_kernel, (rows, block_len, kv_coun...  22.7 us
    unnamed x1, local copies, waits for them, and re-layouts  1.67 us

profile of v1, /device:TPU:97, one launch (start us, length us, event | category | flops | bytes accessed | tf_op | source)
XLA Modules:
  0.0 71.2 jit_solution(12664200153371685930)
XLA Ops:
  0.6 22.7 %attend.1 = (bf16[32,1024,128]{2,1,0:T(8,128)(2,1)}, bf16[32,1024,128]{2,1,0:T(8,128)(2,1)}, f32[8,5,8,128]{3,2,1,0:T(8,128)}, f32[8,4,4096]{2,1,0:T(4,128)}) custom-call(s32[32]{0:T(128)} %pos_ref.1, bf16[32,4096]{1,0:T(8,128)(2,1)} %hid_ref.1, f32[1,4096]{1,0:T(1,128)} %bitcast.8, f32[1,128]{1,0:T(1,128)} %constant.2.clone.freq_ref, ...), custom_call_target="tpu_custom_call" | custom-call | tf_op jit(solution)/shard_map/attend/pallas_call | solution.py:335
  23.3 46.2 %tail.1 = bf16[32,4096]{1,0:T(8,128)(2,1)} custom-call(f32[8,5,8,128]{3,2,1,0:T(8,128)} %get-tuple-element.7.part_ref, f32[8,4,4096]{2,1,0:T(4,128)} %get-tuple-element.8.resid_hbm, f32[1,4096]{1,0:T(1,128)} %bitcast.9, bf16[1024,4096]{1,0:T(8,128)(2,1)} %wo_hbm.1, bf16[4096,7168]{1,0:T(8,128)(2,1)} %wgu_hbm.1, bf16[3584,4096]{1,0:T(8,128)(2,1)} %wd_hbm.1), custom_call_target="tpu_custom_call" | custom-call | tf_op jit(solution)/shard_map/tail/pallas_call | solution.py:365
  69.6 1.7 %copy.15 = bf16[32,4096]{1,0:T(8,128)(2,1)} copy(bf16[32,4096]{1,0:T(8,128)(2,1)} %tail.1) | data formatting | bytes 524288

commit v2 on v1

v2 whole, which is shorter than its diff:
```python
import functools

import jax
import jax.numpy as jnp
import numpy as np
from jax import lax
from jax.experimental import pallas as pl
from jax.experimental.pallas import tpu as pltpu
from jax.sharding import PartitionSpec as P

WINDOW = 2047
ROPE_BASE = 10000.0
NORM_EPS = 1e-5
MESH = pl.DeviceIdType.MESH
LANES = 128
QKV_CHUNKS = 4
CHUNKS = 4
VMEM_LIMIT = 60 * 1024 * 1024
F32, BF16 = jnp.float32, jnp.bfloat16


def dot(lhs, rhs):
    return jnp.dot(lhs, rhs, preferred_element_type=F32)


def dot_t(lhs, rhs):
    return lax.dot_general(lhs, rhs, (((1,), (1,)), ((), ())), preferred_element_type=F32)


def round_bf16(values):
    return values.astype(BF16).astype(F32)


def row_scale(values):
    return lax.rsqrt(jnp.mean(values * values, axis=-1, keepdims=True) + NORM_EPS)


def attend_kernel(dims, pos_hbm, hid_hbm, gain_hbm, freq_hbm, w_hbm, k_hbm, v_hbm, ko_hbm, vo_hbm, part_hbm, resid_hbm,
                  pos_ref, hid_ref, gain_ref, freq_ref, w_buf, k_buf, v_buf, norm_buf, proj_buf, q_buf, new_buf, s_buf,
                  part_ref, resid_ref, in_sem, w_sem, k_sem, v_sem, ko_sem, vo_sem, out_sem):
    rows, block_len, kv_count, group, shares = dims
    heads = kv_count * group
    per_share = rows // shares
    w_rows = w_buf.shape[0] // QKV_CHUNKS

    def w_copy(c):
        part = pl.ds(c * w_rows, w_rows)
        return pltpu.make_async_copy(w_hbm.at[part], w_buf.at[part], w_sem.at[c])

    def cache_copy(src, dst, sem, g):
        part = pl.ds(g * per_share, per_share)
        return pltpu.make_async_copy(src.at[part], dst.at[part], sem.at[g])

    small = [pltpu.make_async_copy(src, dst, in_sem.at[n]) for n, (src, dst) in enumerate(
        [(hid_hbm, hid_ref), (gain_hbm, gain_ref), (freq_hbm, freq_ref), (pos_hbm, pos_ref)])]
    for copy in small:
        copy.start()
    for c in range(QKV_CHUNKS):
        w_copy(c).start()
    for g in range(shares):
        cache_copy(k_hbm, k_buf, k_sem, g).start(priority=1)
    for copy in small:
        copy.wait()

    resid = hid_ref[...].astype(F32)
    for s in range(shares):
        resid_ref[s] = resid[s * per_share:(s + 1) * per_share]
    resid_copy = pltpu.make_async_copy(resid_ref, resid_hbm, out_sem.at[0])
    resid_copy.start()
    norm_buf[...] = (resid * row_scale(resid) * gain_ref[...]).astype(BF16)

    row_id = lax.broadcasted_iota(jnp.int32, (8, LANES), 0)
    tiles = []
    for r in range(rows // 8):
        tile = jnp.zeros((8, LANES), jnp.int32)
        for i in range(8):
            tile = jnp.where(row_id == i, pos_ref[r * 8 + i], tile)
        tiles.append(tile)
    angles = jnp.concatenate(tiles, axis=0).astype(F32) * freq_ref[...]
    cos_tab = jnp.cos(angles)
    sin_tab = jnp.sin(angles)
    lane_id = lax.broadcasted_iota(jnp.int32, (rows, LANES), 1)
    sin_tab = jnp.where(lane_id < LANES // 2, -sin_tab, sin_tab)

    def rope(values):
        return values * cos_tab + pltpu.roll(values, LANES // 2, axis=1) * sin_tab

    for c in range(QKV_CHUNKS):
        part = slice(c * w_rows, (c + 1) * w_rows)
        w_copy(c).wait()
        if c == QKV_CHUNKS - 1:
            for g in range(shares):
                cache_copy(v_hbm, v_buf, v_sem, g).start()
        term = dot(norm_buf[:, part], w_buf[part, :])
        proj_buf[...] = term if c == 0 else proj_buf[...] + term

    for kv in range(kv_count):
        base = kv * (group + 2) * LANES
        for g in range(group):
            q_new = round_bf16(rope(proj_buf[:, base + g * LANES:base + (g + 1) * LANES]))
            q_buf[pl.ds(kv * group + g, rows, stride=heads), :] = q_new
        k_col = base + group * LANES
        new_buf[pl.ds(kv, rows, stride=8), :] = round_bf16(rope(proj_buf[:, k_col:k_col + LANES]))
        new_buf[pl.ds(kv_count + kv, rows, stride=8), :] = round_bf16(proj_buf[:, k_col + LANES:k_col + 2 * LANES])

    start = lax.axis_index('sp') * block_len
    score_scale = LANES ** -0.5
    tile_rows = 8 * kv_count
    tile_id = lax.broadcasted_iota(jnp.int32, (tile_rows, LANES), 0)
    col_id = lax.broadcasted_iota(jnp.int32, (heads, block_len * kv_count), 1)
    head_id = lax.broadcasted_iota(jnp.int32, (heads, block_len * kv_count), 0)
    own_kv = lax.rem(col_id, kv_count) == head_id // group
    slot_id = jnp.where(own_kv, start + col_id // kv_count, -1)
    stat_lane = lax.broadcasted_iota(jnp.int32, (heads, LANES), 1)

    def write_row(buf, b, first):
        slot = pos_ref[b] - start

        @pl.when(jnp.logical_and(slot >= 0, slot < block_len))
        def _():
            base = pl.multiple_of((slot // 8) * tile_rows, tile_rows)
            tile = buf[b, pl.ds(base, tile_rows), :].astype(F32)
            lines = new_buf[pl.ds(pl.multiple_of(b * 8, 8), 8), :]
            new = jnp.zeros((tile_rows, LANES), F32)
            for kv in range(kv_count):
                line = lines[first + kv:first + kv + 1, :]
                new = jnp.where(lax.rem(tile_id, kv_count) == kv, line, new)
            hit = tile_id // kv_count == lax.rem(slot, 8)
            buf[b, pl.ds(base, tile_rows), :] = jnp.where(hit, new, tile).astype(BF16)

    def key_step(g, carry):
        cache_copy(k_hbm, k_buf, k_sem, g).wait()
        for i in range(per_share):
            write_row(k_buf, g * per_share + i, 0)
        cache_copy(k_buf, ko_hbm, ko_sem, g).start(priority=1)
        for i in range(per_share):
            b = g * per_share + i
            q_rows = q_buf[pl.ds(pl.multiple_of(b * heads, heads), heads), :].astype(BF16)
            s_buf[b] = dot_t(q_rows, k_buf[b])
        return carry

    def weight_step(g, carry):
        stats = jnp.zeros((heads, LANES), F32)
        for i in range(per_share):
            b = g * per_share + i
            pos = pos_ref[b]
            seen = (slot_id <= pos) & (slot_id >= jnp.maximum(pos - WINDOW, 0))
            scores = jnp.where(seen, s_buf[b] * score_scale, -jnp.inf)
            top = jnp.max(scores, axis=-1, keepdims=True)
            base = jnp.where(top == -jnp.inf, 0.0, top)
            weights = jnp.exp(scores - base)
            total = jnp.sum(weights, axis=-1, keepdims=True)
            s_buf[b] = weights
            stats = jnp.where(stat_lane == i, top, stats)
            stats = jnp.where(stat_lane == per_share + i, total, stats)
        part_ref[g, per_share] = stats
        return carry

    def value_step(g, carry):
        cache_copy(v_hbm, v_buf, v_sem, g).wait()
        for i in range(per_share):
            write_row(v_buf, g * per_share + i, kv_count)
        cache_copy(v_buf, vo_hbm, vo_sem, g).start(priority=1)
        for i in range(per_share):
            b = g * per_share + i
            part_ref[g, i] = dot(s_buf[b].astype(BF16), v_buf[b])
        return carry

    lax.fori_loop(0, shares, key_step, 0)
    lax.fori_loop(0, shares, weight_step, 0)
    lax.fori_loop(0, shares, value_step, 0)
    part_copy = pltpu.make_async_copy(part_ref, part_hbm, out_sem.at[1])
    part_copy.start()
    for g in range(shares):
        cache_copy(k_buf, ko_hbm, ko_sem, g).wait()
        cache_copy(v_buf, vo_hbm, vo_sem, g).wait()
    resid_copy.wait()
    part_copy.wait()


def tail_kernel(n_tp, n_sp, part_ref, resid_hbm, gain_ref, wo_hbm, wgu_hbm, wd_hbm, out_ref,
                wo_buf, wgu_buf, wd_buf, resid_buf, part_in, att_buf, y1_buf, x1_in, x1_buf, r2_buf,
                a_out, a_in, y2_buf, x2_in, w_sem, b_send, b_recv, y1_send, y1_recv, g1_send, g1_recv,
                a_send, a_recv, y2_send, y2_recv, g2_send, g2_recv):
    t = lax.axis_index('tp')
    s = lax.axis_index('sp')
    n_chip = n_sp // 2
    chip, core = s // 2, lax.rem(s, 2)
    mate = chip * 2 + 1 - core
    units, model = wd_hbm.shape
    chip_units = units // n_chip
    splits = unit_splits(chip_units)
    half = model // 2
    per_share = part_ref.shape[1] - 1
    heads = part_ref.shape[2]
    half_rows = n_chip * per_share
    group_rows = 2 * per_share

    def group_of(dev):
        return lax.rem(dev, 2) * n_chip + dev // 2

    resid_load = pltpu.make_async_copy(resid_hbm.at[group_of(s)], resid_buf, w_sem.at[0])
    wo_load = pltpu.make_async_copy(wo_hbm, wo_buf, w_sem.at[1])
    gu_loads = []
    at = 0
    for first, width in splits:
        for side in range(2):
            col = pl.multiple_of(side * units + chip * chip_units + first, LANES)
            gu_loads.append(pltpu.make_async_copy(wgu_hbm.at[:, pl.ds(col, width)], wgu_buf.at[:, pl.ds(at, width)], w_sem.at[2 + len(gu_loads)]))
            at += width
    wd_col = pl.multiple_of(lax.rem(chip, 2) * half, half)
    wd_load = pltpu.make_async_copy(wd_hbm.at[:, pl.ds(wd_col, half)], wd_buf, w_sem.at[6])
    resid_load.start()
    wo_load.start()

    def wrap(value, count):
        return lax.rem(value + count, count)

    barrier = pltpu.get_barrier_semaphore()
    for k in range(1, n_sp):
        pl.semaphore_signal(barrier, inc=1, device_id={'sp': wrap(s + k, n_sp)}, device_id_type=MESH)
    for k in range(1, n_tp):
        pl.semaphore_signal(barrier, inc=1, device_id={'tp': wrap(t + k, n_tp)}, device_id_type=MESH)
    pl.semaphore_wait(barrier, n_sp + n_tp - 2)

    sent = []

    def push(src, dst, send, recv, device):
        copy = pltpu.make_async_remote_copy(src_ref=src, dst_ref=dst, send_sem=send, recv_sem=recv, device_id=device, device_id_type=MESH)
        copy.start()
        sent.append(copy)

    def arrive(dst, recv):
        pltpu.make_async_remote_copy(src_ref=dst, dst_ref=dst, send_sem=b_send.at[0], recv_sem=recv, device_id={'sp': mate}, device_id_type=MESH).wait_recv()

    near_first = sorted(range(1, n_chip), key=lambda k: min(k, n_chip - k))

    def peer(k):
        return {'sp': wrap(chip + k, n_chip) * 2 + core}

    for k in range(1, n_sp):
        dev = wrap(s + k, n_sp)
        push(part_ref.at[group_of(dev)], part_in.at[s], b_send.at[k - 1], b_recv.at[k - 1], {'sp': dev})
    part_in[s] = part_ref[group_of(s)]
    resid_load.wait()
    wo_load.wait()
    for load in gu_loads:
        load.start()
    for k in range(1, n_sp):
        arrive(part_in.at[wrap(s - k, n_sp)], b_recv.at[k - 1])
    stats = [part_in[j, per_share] for j in range(n_sp)]
    top = functools.reduce(jnp.maximum, stats)
    scales = [jnp.exp(st - top) for st in stats]
    total = sum(sc * pltpu.roll(st, LANES - per_share, axis=1) for sc, st in zip(scales, stats))
    for i in range(per_share):
        acc = sum(part_in[j, i] * scales[j][:, i:i + 1] for j in range(n_sp))
        att_buf[i * heads:(i + 1) * heads, :] = round_bf16(acc / total[:, i:i + 1])
    attended = jnp.concatenate([att_buf[pl.ds(h, per_share, stride=heads), :] for h in range(heads)], axis=1).astype(BF16)

    width = model // CHUNKS
    for n in range(CHUNKS):
        y1_buf[n, t] = round_bf16(dot(attended, wo_buf[:, n * width:(n + 1) * width]))
        for k in range(1, n_tp):
            push(y1_buf.at[n, t], y1_buf.at[n, t], y1_send.at[n, k - 1], y1_recv.at[n, k - 1], {'tp': wrap(t + k, n_tp)})
    wd_load.start()
    for n in range(CHUNKS):
        for k in range(1, n_tp):
            arrive(y1_buf.at[n, wrap(t - k, n_tp)], y1_recv.at[n, k - 1])
        out_sum = functools.reduce(jnp.add, [y1_buf[n, j] for j in range(n_tp)])
        x1_in[n, chip] = resid_buf[:, n * width:(n + 1) * width] + out_sum
        for k in near_first:
            push(x1_in.at[n, chip], x1_in.at[n, chip], g1_send.at[n, k - 1], g1_recv.at[n, k - 1], peer(k))
    square = jnp.zeros((half_rows, LANES), F32)
    for n in range(CHUNKS):
        for k in near_first:
            arrive(x1_in.at[n, wrap(chip - k, n_chip)], g1_recv.at[n, k - 1])
        for j in range(n_chip):
            x1_buf[j * per_share:(j + 1) * per_share, n * width:(n + 1) * width] = x1_in[n, j]
        for c in range(width // LANES):
            piece = x1_buf[:, n * width + c * LANES:n * width + (c + 1) * LANES]
            square = square + piece * piece
    scale = lax.rsqrt(jnp.sum(square, axis=-1, keepdims=True) / model + NORM_EPS)
    for c in range(0, model, 4 * LANES):
        part = slice(c, c + 4 * LANES)
        r2_buf[:, part] = (x1_buf[:, part] * scale * gain_ref[:, part]).astype(BF16)

    at = 0
    for n, (first, width) in enumerate(splits):
        gu_loads[2 * n].wait()
        gu_loads[2 * n + 1].wait()
        both = dot(r2_buf[...], wgu_buf[:, at:at + 2 * width])
        at += 2 * width
        gate = both[:, :width]
        act = round_bf16(gate * jax.nn.sigmoid(gate) * both[:, width:])
        for j in range(half_rows // group_rows):
            a_out[j, :, first:first + width] = act[j * group_rows:(j + 1) * group_rows]
        for k in near_first:
            dst = wrap(chip + k, n_chip)
            push(a_out.at[dst // 2, :, pl.ds(first, width)], a_in.at[chip, :, pl.ds(first, width)],
                 a_send.at[n, k - 1], a_recv.at[n, k - 1], peer(k))
    a_in[chip] = a_out[chip // 2]
    wd_load.wait()
    for n, (first, width) in enumerate(splits):
        for k in near_first:
            arrive(a_in.at[wrap(chip - k, n_chip), :, pl.ds(first, width)], a_recv.at[n, k - 1])
    act_rows = jnp.concatenate([a_in[j] for j in range(n_chip)], axis=1).astype(BF16)

    width = half // CHUNKS
    for n in range(CHUNKS):
        y2_buf[n, t] = round_bf16(dot(act_rows, wd_buf[:, n * width:(n + 1) * width]))
        for k in range(1, n_tp):
            push(y2_buf.at[n, t], y2_buf.at[n, t], y2_send.at[n, k - 1], y2_recv.at[n, k - 1], {'tp': wrap(t + k, n_tp)})
    own_rows = pl.ds(pl.multiple_of(chip // 2 * group_rows, group_rows), group_rows)
    for n in range(CHUNKS):
        for k in range(1, n_tp):
            arrive(y2_buf.at[n, wrap(t - k, n_tp)], y2_recv.at[n, k - 1])
        down_sum = functools.reduce(jnp.add, [y2_buf[n, j] for j in range(n_tp)])
        x2_in[n, s] = x1_buf[own_rows, pl.ds(pl.multiple_of(wd_col + n * width, width), width)] + down_sum
        for k in near_first:
            push(x2_in.at[n, s], x2_in.at[n, s], g2_send.at[n, k], g2_recv.at[n, k], peer(k))
        push(x2_in.at[n, s], x2_in.at[n, s], g2_send.at[n, 0], g2_recv.at[n, 0], {'sp': mate})
    for n in range(CHUNKS):
        for k in near_first:
            far = x2_in.at[n, wrap(chip - k, n_chip) * 2 + core]
            arrive(far, g2_recv.at[n, k])
            push(far, far, g2_send.at[n, n_chip + k - 1], g2_recv.at[n, n_chip + k - 1], {'sp': mate})
    for n in range(CHUNKS):
        arrive(x2_in.at[n, mate], g2_recv.at[n, 0])
        for k in near_first:
            arrive(x2_in.at[n, wrap(chip - k, n_chip) * 2 + 1 - core], g2_recv.at[n, n_chip + k - 1])
        for c in range(2):
            for side in range(2):
                lines = jnp.concatenate([x2_in[n, 2 * j + c] for j in range(side, n_chip, 2)], axis=0)
                col = side * half + n * width
                out_ref[c * half_rows:(c + 1) * half_rows, col:col + width] = lines.astype(BF16)
    for copy in sent:
        copy.wait_send()


def unit_splits(count):
    first = (count // LANES + 1) // 2 * LANES
    return [(0, first), (first, count - first)]


def vmem():
    return pl.BlockSpec(memory_space=pltpu.VMEM)


def hbm():
    return pl.BlockSpec(memory_space=pl.ANY)


def solution(mesh):
    n_tp, n_sp = mesh.shape['tp'], mesh.shape['sp']
    cache_spec = P('dp', 'sp', 'tp', None)

    def local_step(hidden, positions, norm_attn, norm_mlp, w_qkv, w_out, w_gate_up, w_down, k_cache, v_cache):
        rows, block_len, kv_count, head_dim = k_cache.shape
        model = hidden.shape[1]
        group = w_qkv.shape[1] // (kv_count * head_dim) - 2
        heads = kv_count * group
        shares = n_sp
        per_share = rows // shares
        flat = (rows, block_len * kv_count, head_dim)
        inv_freq = ROPE_BASE ** (-np.arange(0, head_dim, 2) / head_dim)
        freq = jnp.asarray(np.concatenate([inv_freq, inv_freq])[None, :], F32)
        dma = pltpu.SemaphoreType.DMA

        k_upd, v_upd, parts, resid = pl.pallas_call(
            functools.partial(attend_kernel, (rows, block_len, kv_count, group, shares)),
            out_shape=(
                jax.ShapeDtypeStruct(flat, BF16),
                jax.ShapeDtypeStruct(flat, BF16),
                jax.ShapeDtypeStruct((shares, per_share + 1, heads, head_dim), F32),
                jax.ShapeDtypeStruct((shares, per_share, model), F32),
            ),
            in_specs=[hbm()] * 7,
            out_specs=(hbm(), hbm(), hbm(), hbm()),
            scratch_shapes=[
                pltpu.SMEM(positions.shape, jnp.int32),
                pltpu.VMEM(hidden.shape, BF16),
                pltpu.VMEM((1, model), F32),
                pltpu.VMEM(freq.shape, F32),
                pltpu.VMEM(w_qkv.shape, BF16),
                pltpu.VMEM(flat, BF16),
                pltpu.VMEM(flat, BF16),
                pltpu.VMEM((rows, model), BF16),
                pltpu.VMEM((rows, w_qkv.shape[1]), F32),
                pltpu.VMEM((rows * heads, head_dim), F32),
                pltpu.VMEM((rows * 8, head_dim), F32),
                pltpu.VMEM((rows, heads, block_len * kv_count), F32),
                pltpu.VMEM((shares, per_share + 1, heads, head_dim), F32),
                pltpu.VMEM((shares, per_share, model), F32),
                dma((4,)), dma((QKV_CHUNKS,)), dma((shares,)), dma((shares,)), dma((shares,)), dma((shares,)), dma((2,)),
            ],
            compiler_params=pltpu.CompilerParams(vmem_limit_bytes=VMEM_LIMIT),
            name='attend',
        )(positions, hidden, norm_attn[None, :], freq, w_qkv, k_cache.reshape(flat), v_cache.reshape(flat))

        units = w_down.shape[0]
        n_chip = n_sp // 2
        half_rows, group_rows, half = rows // 2, 2 * per_share, model // 2
        result = pl.pallas_call(
            functools.partial(tail_kernel, n_tp, n_sp),
            out_shape=jax.ShapeDtypeStruct((rows, model), BF16),
            in_specs=[vmem(), hbm(), vmem(), hbm(), hbm(), hbm()],
            out_specs=vmem(),
            scratch_shapes=[
                pltpu.VMEM(w_out.shape, BF16),
                pltpu.VMEM((model, 2 * units // n_chip), BF16),
                pltpu.VMEM((units, half), BF16),
                pltpu.VMEM((per_share, model), F32),
                pltpu.VMEM((n_sp, per_share + 1, heads, head_dim), F32),
                pltpu.VMEM((per_share * heads, head_dim), F32),
                pltpu.VMEM((CHUNKS, n_tp, per_share, model // CHUNKS), F32),
                pltpu.VMEM((CHUNKS, n_chip, per_share, model // CHUNKS), F32),
                pltpu.VMEM((half_rows, model), F32),
                pltpu.VMEM((half_rows, model), BF16),
                pltpu.VMEM((half_rows // group_rows, group_rows, units // n_chip), F32),
                pltpu.VMEM((n_chip, group_rows, units // n_chip), F32),
                pltpu.VMEM((CHUNKS, n_tp, group_rows, half // CHUNKS), F32),
                pltpu.VMEM((CHUNKS, n_sp, group_rows, half // CHUNKS), F32),
                dma((7,)),
                dma((n_sp - 1,)), dma((n_sp - 1,)),
                dma((CHUNKS, n_tp - 1)), dma((CHUNKS, n_tp - 1)),
                dma((CHUNKS, n_chip - 1)), dma((CHUNKS, n_chip - 1)),
                dma((2, n_chip - 1)), dma((2, n_chip - 1)),
                dma((CHUNKS, n_tp - 1)), dma((CHUNKS, n_tp - 1)),
                dma((CHUNKS, n_sp - 1)), dma((CHUNKS, n_sp - 1)),
            ],
            compiler_params=pltpu.CompilerParams(vmem_limit_bytes=VMEM_LIMIT, collective_id=0, has_side_effects=True),
            name='tail',
        )(parts, resid, norm_mlp[None, :], w_out, w_gate_up, w_down)
        return result, k_upd.reshape(k_cache.shape), v_upd.reshape(v_cache.shape)

    return jax.shard_map(local_step, mesh=mesh, in_specs=(P('dp', None), P('dp'), P(None), P(None), P(None, 'tp'), P('tp', None), P(None, 'tp'), P('tp', None), cache_spec, cache_spec), out_specs=(P('dp', None), cache_spec, cache_spec), check_vma=False)
```

time: 71.4 us -> 61.9 us (0.87)
  Pallas kernels: 68.9 us -> 59.4 us
    pallas_call x1, Pallas kernels: 22.7 us -> 17.8 us  [local_step(): pl.pallas_call(functools.partial(attend_kernel, (rows, block_len, kv_coun...]
    pallas_call x1, Pallas kernels: 46.2 us -> 41.7 us  [local_step(): pl.pallas_call(functools.partial(tail_kernel, n_tp, n_sp), out_shape=jax....]
where the time goes in v2:
time: 61.9 us; the launch traced here: 61.7 us
  Pallas kernels  59.4 us (96%)
  local copies, waits for them, and re-layouts  1.67 us (3%)
  between operations  0.65 us (1%)
    pallas_call x1, Pallas kernels, local_step(): pl.pallas_call(functools.partial(tail_kernel, n_tp, n_sp), out_shape=jax....  41.7 us
    pallas_call x1, Pallas kernels, local_step(): pl.pallas_call(functools.partial(attend_kernel, (rows, block_len, kv_coun...  17.8 us
    unnamed x1, local copies, waits for them, and re-layouts  1.67 us

profile of v2, /device:TPU:97, one launch (start us, length us, event | category | flops | bytes accessed | tf_op | source)
XLA Modules:
  0.0 61.7 jit_solution(1036922862667337750)
XLA Ops:
  0.6 17.8 %attend.1 = (bf16[32,1024,128]{2,1,0:T(8,128)(2,1)}, bf16[32,1024,128]{2,1,0:T(8,128)(2,1)}, f32[8,5,8,128]{3,2,1,0:T(8,128)}, f32[8,4,4096]{2,1,0:T(4,128)}) custom-call(s32[32]{0:T(128)} %pos_hbm.1, bf16[32,4096]{1,0:T(8,128)(2,1)} %hid_hbm.1, f32[1,4096]{1,0:T(1,128)} %bitcast.8, f32[1,128]{1,0:T(1,128)} %constant.2.clone.freq_hbm, ...), custom_call_target="tpu_custom_call" | custom-call | tf_op jit(solution)/shard_map/attend/pallas_call | solution.py:369
  18.4 41.7 %tail.1 = bf16[32,4096]{1,0:T(8,128)(2,1)} custom-call(f32[8,5,8,128]{3,2,1,0:T(8,128)} %get-tuple-element.7.part_ref, f32[8,4,4096]{2,1,0:T(4,128)} %get-tuple-element.8.resid_hbm, f32[1,4096]{1,0:T(1,128)} %bitcast.9, bf16[1024,4096]{1,0:T(8,128)(2,1)} %wo_hbm.1, bf16[4096,7168]{1,0:T(8,128)(2,1)} %wgu_hbm.1, bf16[3584,4096]{1,0:T(8,128)(2,1)} %wd_hbm.1), custom_call_target="tpu_custom_call" | custom-call | tf_op jit(solution)/shard_map/tail/pallas_call | solution.py:403
  60.1 1.7 %copy.15 = bf16[32,4096]{1,0:T(8,128)(2,1)} copy(bf16[32,4096]{1,0:T(8,128)(2,1)} %tail.1) | data formatting | bytes 524288

commit v3 on v2

--- a/solution.py
+++ b/solution.py
@@ -15,6 +15,7 @@
 LANES = 128
 QKV_CHUNKS = 4
 CHUNKS = 4
+GU_SPLITS = 2
 VMEM_LIMIT = 60 * 1024 * 1024
 F32, BF16 = jnp.float32, jnp.bfloat16
 
@@ -58,13 +59,13 @@
     for c in range(QKV_CHUNKS):
         w_copy(c).start()
     for g in range(shares):
-        cache_copy(k_hbm, k_buf, k_sem, g).start(priority=1)
+        cache_copy(k_hbm, k_buf, k_sem, g).start()
     for copy in small:
         copy.wait()
 
     resid = hid_ref[...].astype(F32)
-    for s in range(shares):
-        resid_ref[s] = resid[s * per_share:(s + 1) * per_share]
+    for n in range(resid_ref.shape[0]):
+        resid_ref[n] = resid[n * 2 * per_share:(n + 1) * 2 * per_share]
     resid_copy = pltpu.make_async_copy(resid_ref, resid_hbm, out_sem.at[0])
     resid_copy.start()
     norm_buf[...] = (resid * row_scale(resid) * gain_ref[...]).astype(BF16)
@@ -132,7 +133,7 @@
         cache_copy(k_hbm, k_buf, k_sem, g).wait()
         for i in range(per_share):
             write_row(k_buf, g * per_share + i, 0)
-        cache_copy(k_buf, ko_hbm, ko_sem, g).start(priority=1)
+        cache_copy(k_buf, ko_hbm, ko_sem, g).start()
         for i in range(per_share):
             b = g * per_share + i
             q_rows = q_buf[pl.ds(pl.multiple_of(b * heads, heads), heads), :].astype(BF16)
@@ -160,7 +161,7 @@
         cache_copy(v_hbm, v_buf, v_sem, g).wait()
         for i in range(per_share):
             write_row(v_buf, g * per_share + i, kv_count)
-        cache_copy(v_buf, vo_hbm, vo_sem, g).start(priority=1)
+        cache_copy(v_buf, vo_hbm, vo_sem, g).start()
         for i in range(per_share):
             b = g * per_share + i
             part_ref[g, i] = dot(s_buf[b].astype(BF16), v_buf[b])
@@ -179,37 +180,41 @@
 
 
 def tail_kernel(n_tp, n_sp, part_ref, resid_hbm, gain_ref, wo_hbm, wgu_hbm, wd_hbm, out_ref,
-                wo_buf, wgu_buf, wd_buf, resid_buf, part_in, att_buf, y1_buf, x1_in, x1_buf, r2_buf,
-                a_out, a_in, y2_buf, x2_in, w_sem, b_send, b_recv, y1_send, y1_recv, g1_send, g1_recv,
-                a_send, a_recv, y2_send, y2_recv, g2_send, g2_recv):
+                wo_buf, wgu_buf, wd_own, wd_mate, resid_buf, part_in, att_buf, y1_buf, x1_in, r2_buf,
+                z_out, z_in, y2_buf, x2_in, w_sem, b_send, b_recv, m_send, m_recv, y1_send, y1_recv,
+                y2_send, y2_recv, g2_send, g2_recv):
     t = lax.axis_index('tp')
     s = lax.axis_index('sp')
     n_chip = n_sp // 2
     chip, core = s // 2, lax.rem(s, 2)
-    mate = chip * 2 + 1 - core
+    other = 1 - core
+    mate = chip * 2 + other
     units, model = wd_hbm.shape
-    chip_units = units // n_chip
-    splits = unit_splits(chip_units)
+    core_units = units // 2
+    split = core_units // GU_SPLITS
     half = model // 2
+    width = half // CHUNKS
     per_share = part_ref.shape[1] - 1
     heads = part_ref.shape[2]
-    half_rows = n_chip * per_share
-    group_rows = 2 * per_share
-
-    def group_of(dev):
-        return lax.rem(dev, 2) * n_chip + dev // 2
-
-    resid_load = pltpu.make_async_copy(resid_hbm.at[group_of(s)], resid_buf, w_sem.at[0])
-    wo_load = pltpu.make_async_copy(wo_hbm, wo_buf, w_sem.at[1])
+    share_rows = per_share * heads
+    rows = 2 * per_share
+
+    def columns(which, size):
+        return pl.ds(pl.multiple_of(which * size, LANES), size)
+
+    resid_load = pltpu.make_async_copy(resid_hbm.at[chip, :, columns(core, half)], resid_buf, w_sem.at[0])
+    wo_load = pltpu.make_async_copy(wo_hbm.at[:, columns(core, half)], wo_buf, w_sem.at[1])
     gu_loads = []
-    at = 0
-    for first, width in splits:
+    for n in range(GU_SPLITS):
         for side in range(2):
-            col = pl.multiple_of(side * units + chip * chip_units + first, LANES)
-            gu_loads.append(pltpu.make_async_copy(wgu_hbm.at[:, pl.ds(col, width)], wgu_buf.at[:, pl.ds(at, width)], w_sem.at[2 + len(gu_loads)]))
-            at += width
-    wd_col = pl.multiple_of(lax.rem(chip, 2) * half, half)
-    wd_load = pltpu.make_async_copy(wd_hbm.at[:, pl.ds(wd_col, half)], wd_buf, w_sem.at[6])
+            col = pl.multiple_of(side * units + core * core_units + n * split, LANES)
+            at = (2 * n + side) * split
+            gu_loads.append(pltpu.make_async_copy(wgu_hbm.at[:, pl.ds(col, split)], wgu_buf.at[:, pl.ds(at, split)], w_sem.at[4 + len(gu_loads)]))
+    wd_rows = columns(core, core_units)
+    wd_loads = [
+        pltpu.make_async_copy(wd_hbm.at[wd_rows, columns(other, half)], wd_mate, w_sem.at[2]),
+        pltpu.make_async_copy(wd_hbm.at[wd_rows, columns(core, half)], wd_own, w_sem.at[3]),
+    ]
     resid_load.start()
     wo_load.start()
 
@@ -233,18 +238,17 @@
     def arrive(dst, recv):
         pltpu.make_async_remote_copy(src_ref=dst, dst_ref=dst, send_sem=b_send.at[0], recv_sem=recv, device_id={'sp': mate}, device_id_type=MESH).wait_recv()
 
+    to_mate = {'sp': mate}
     near_first = sorted(range(1, n_chip), key=lambda k: min(k, n_chip - k))
-
-    def peer(k):
-        return {'sp': wrap(chip + k, n_chip) * 2 + core}
+    far_first = near_first[::-1]
 
     for k in range(1, n_sp):
         dev = wrap(s + k, n_sp)
-        push(part_ref.at[group_of(dev)], part_in.at[s], b_send.at[k - 1], b_recv.at[k - 1], {'sp': dev})
-    part_in[s] = part_ref[group_of(s)]
+        push(part_ref.at[dev], part_in.at[s], b_send.at[k - 1], b_recv.at[k - 1], {'sp': dev})
+    part_in[s] = part_ref[s]
     resid_load.wait()
     wo_load.wait()
-    for load in gu_loads:
+    for load in gu_loads[:2]:
         load.start()
     for k in range(1, n_sp):
         arrive(part_in.at[wrap(s - k, n_sp)], b_recv.at[k - 1])
@@ -254,92 +258,83 @@
     total = sum(sc * pltpu.roll(st, LANES - per_share, axis=1) for sc, st in zip(scales, stats))
     for i in range(per_share):
         acc = sum(part_in[j, i] * scales[j][:, i:i + 1] for j in range(n_sp))
-        att_buf[i * heads:(i + 1) * heads, :] = round_bf16(acc / total[:, i:i + 1])
-    attended = jnp.concatenate([att_buf[pl.ds(h, per_share, stride=heads), :] for h in range(heads)], axis=1).astype(BF16)
-
-    width = model // CHUNKS
+        at = pl.multiple_of(core * share_rows + i * heads, heads)
+        att_buf[pl.ds(at, heads), :] = round_bf16(acc / total[:, i:i + 1])
+    mine = att_buf.at[pl.ds(pl.multiple_of(core * share_rows, heads), share_rows)]
+    push(mine, mine, m_send.at[0], m_recv.at[0], to_mate)
+    for load in gu_loads[2:]:
+        load.start()
+    arrive(att_buf.at[pl.ds(pl.multiple_of(other * share_rows, heads), share_rows)], m_recv.at[0])
+    attended = jnp.concatenate([att_buf[pl.ds(h, rows, stride=heads), :] for h in range(heads)], axis=1).astype(BF16)
+
     for n in range(CHUNKS):
         y1_buf[n, t] = round_bf16(dot(attended, wo_buf[:, n * width:(n + 1) * width]))
         for k in range(1, n_tp):
             push(y1_buf.at[n, t], y1_buf.at[n, t], y1_send.at[n, k - 1], y1_recv.at[n, k - 1], {'tp': wrap(t + k, n_tp)})
-    wd_load.start()
+    for load in wd_loads:
+        load.start()
     for n in range(CHUNKS):
         for k in range(1, n_tp):
             arrive(y1_buf.at[n, wrap(t - k, n_tp)], y1_recv.at[n, k - 1])
         out_sum = functools.reduce(jnp.add, [y1_buf[n, j] for j in range(n_tp)])
-        x1_in[n, chip] = resid_buf[:, n * width:(n + 1) * width] + out_sum
-        for k in near_first:
-            push(x1_in.at[n, chip], x1_in.at[n, chip], g1_send.at[n, k - 1], g1_recv.at[n, k - 1], peer(k))
-    square = jnp.zeros((half_rows, LANES), F32)
-    for n in range(CHUNKS):
-        for k in near_first:
-            arrive(x1_in.at[n, wrap(chip - k, n_chip)], g1_recv.at[n, k - 1])
-        for j in range(n_chip):
-            x1_buf[j * per_share:(j + 1) * per_share, n * width:(n + 1) * width] = x1_in[n, j]
-        for c in range(width // LANES):
-            piece = x1_buf[:, n * width + c * LANES:n * width + (c + 1) * LANES]
-            square = square + piece * piece
+        x1_in[core, n] = resid_buf[:, n * width:(n + 1) * width] + out_sum
+        push(x1_in.at[core, n], x1_in.at[core, n], m_send.at[1 + n], m_recv.at[1 + n], to_mate)
+    square = jnp.zeros((rows, LANES), F32)
+    for n in range(CHUNKS):
+        arrive(x1_in.at[other, n], m_recv.at[1 + n])
+        for c in range(2):
+            for at in range(0, width, LANES):
+                piece = x1_in[c, n, :, at:at + LANES]
+                square = square + piece * piece
     scale = lax.rsqrt(jnp.sum(square, axis=-1, keepdims=True) / model + NORM_EPS)
-    for c in range(0, model, 4 * LANES):
-        part = slice(c, c + 4 * LANES)
-        r2_buf[:, part] = (x1_buf[:, part] * scale * gain_ref[:, part]).astype(BF16)
-
-    at = 0
-    for n, (first, width) in enumerate(splits):
+    for c in range(2):
+        for n in range(CHUNKS):
+            part = slice(c * half + n * width, c * half + (n + 1) * width)
+            r2_buf[:, part] = (x1_in[c, n] * scale * gain_ref[:, part]).astype(BF16)
+
+    acts = []
+    for n in range(GU_SPLITS):
         gu_loads[2 * n].wait()
         gu_loads[2 * n + 1].wait()
-        both = dot(r2_buf[...], wgu_buf[:, at:at + 2 * width])
-        at += 2 * width
-        gate = both[:, :width]
-        act = round_bf16(gate * jax.nn.sigmoid(gate) * both[:, width:])
-        for j in range(half_rows // group_rows):
-            a_out[j, :, first:first + width] = act[j * group_rows:(j + 1) * group_rows]
-        for k in near_first:
-            dst = wrap(chip + k, n_chip)
-            push(a_out.at[dst // 2, :, pl.ds(first, width)], a_in.at[chip, :, pl.ds(first, width)],
-                 a_send.at[n, k - 1], a_recv.at[n, k - 1], peer(k))
-    a_in[chip] = a_out[chip // 2]
-    wd_load.wait()
-    for n, (first, width) in enumerate(splits):
-        for k in near_first:
-            arrive(a_in.at[wrap(chip - k, n_chip), :, pl.ds(first, width)], a_recv.at[n, k - 1])
-    act_rows = jnp.concatenate([a_in[j] for j in range(n_chip)], axis=1).astype(BF16)
-
-    width = half // CHUNKS
-    for n in range(CHUNKS):
-        y2_buf[n, t] = round_bf16(dot(act_rows, wd_buf[:, n * width:(n + 1) * width]))
+        both = dot(r2_buf[...], wgu_buf[:, 2 * n * split:2 * (n + 1) * split])
+        gate = both[:, :split]
+        acts.append((gate * jax.nn.sigmoid(gate) * both[:, split:]).astype(BF16))
+    act = jnp.concatenate(acts, axis=1)
+    wd_loads[0].wait()
+    for n in range(CHUNKS):
+        z_out[n] = dot(act, wd_mate[:, n * width:(n + 1) * width])
+        push(z_out.at[n], z_in.at[n], m_send.at[1 + CHUNKS + n], m_recv.at[1 + CHUNKS + n], to_mate)
+    wd_loads[1].wait()
+    for n in range(CHUNKS):
+        own = dot(act, wd_own[:, n * width:(n + 1) * width])
+        arrive(z_in.at[n], m_recv.at[1 + CHUNKS + n])
+        y2_buf[n, t] = round_bf16(own + z_in[n])
         for k in range(1, n_tp):
             push(y2_buf.at[n, t], y2_buf.at[n, t], y2_send.at[n, k - 1], y2_recv.at[n, k - 1], {'tp': wrap(t + k, n_tp)})
-    own_rows = pl.ds(pl.multiple_of(chip // 2 * group_rows, group_rows), group_rows)
     for n in range(CHUNKS):
         for k in range(1, n_tp):
             arrive(y2_buf.at[n, wrap(t - k, n_tp)], y2_recv.at[n, k - 1])
         down_sum = functools.reduce(jnp.add, [y2_buf[n, j] for j in range(n_tp)])
-        x2_in[n, s] = x1_buf[own_rows, pl.ds(pl.multiple_of(wd_col + n * width, width), width)] + down_sum
-        for k in near_first:
-            push(x2_in.at[n, s], x2_in.at[n, s], g2_send.at[n, k], g2_recv.at[n, k], peer(k))
-        push(x2_in.at[n, s], x2_in.at[n, s], g2_send.at[n, 0], g2_recv.at[n, 0], {'sp': mate})
+        x2_in[n, s] = x1_in[core, n] + down_sum
+        for k in far_first:
+            push(x2_in.at[n, s], x2_in.at[n, s], g2_send.at[n, k], g2_recv.at[n, k], {'sp': wrap(chip + k, n_chip) * 2 + core})
+        push(x2_in.at[n, s], x2_in.at[n, s], g2_send.at[n, 0], g2_recv.at[n, 0], to_mate)
     for n in range(CHUNKS):
         for k in near_first:
             far = x2_in.at[n, wrap(chip - k, n_chip) * 2 + core]
             arrive(far, g2_recv.at[n, k])
-            push(far, far, g2_send.at[n, n_chip + k - 1], g2_recv.at[n, n_chip + k - 1], {'sp': mate})
+            push(far, far, g2_send.at[n, n_chip + k - 1], g2_recv.at[n, n_chip + k - 1], to_mate)
     for n in range(CHUNKS):
         arrive(x2_in.at[n, mate], g2_recv.at[n, 0])
         for k in near_first:
-            arrive(x2_in.at[n, wrap(chip - k, n_chip) * 2 + 1 - core], g2_recv.at[n, n_chip + k - 1])
-        for c in range(2):
-            for side in range(2):
-                lines = jnp.concatenate([x2_in[n, 2 * j + c] for j in range(side, n_chip, 2)], axis=0)
-                col = side * half + n * width
-                out_ref[c * half_rows:(c + 1) * half_rows, col:col + width] = lines.astype(BF16)
+            arrive(x2_in.at[n, wrap(chip - k, n_chip) * 2 + other], g2_recv.at[n, n_chip + k - 1])
+        for j in range(0, n_chip, 2):
+            for c in range(2):
+                lines = jnp.concatenate([x2_in[n, 2 * j + c], x2_in[n, 2 * j + 2 + c]], axis=0)
+                col = c * half + n * width
+                out_ref[j * rows:(j + 2) * rows, col:col + width] = lines.astype(BF16)
     for copy in sent:
         copy.wait_send()
-
-
-def unit_splits(count):
-    first = (count // LANES + 1) // 2 * LANES
-    return [(0, first), (first, count - first)]
 
 
 def vmem():
@@ -372,7 +367,7 @@
                 jax.ShapeDtypeStruct(flat, BF16),
                 jax.ShapeDtypeStruct(flat, BF16),
                 jax.ShapeDtypeStruct((shares, per_share + 1, heads, head_dim), F32),
-                jax.ShapeDtypeStruct((shares, per_share, model), F32),
+                jax.ShapeDtypeStruct((shares // 2, 2 * per_share, model), F32),
             ),
             in_specs=[hbm()] * 7,
             out_specs=(hbm(), hbm(), hbm(), hbm()),
@@ -390,7 +385,7 @@
                 pltpu.VMEM((rows * 8, head_dim), F32),
                 pltpu.VMEM((rows, heads, block_len * kv_count), F32),
                 pltpu.VMEM((shares, per_share + 1, heads, head_dim), F32),
-                pltpu.VMEM((shares, per_share, model), F32),
+                pltpu.VMEM((shares // 2, 2 * per_share, model), F32),
                 dma((4,)), dma((QKV_CHUNKS,)), dma((shares,)), dma((shares,)), dma((shares,)), dma((shares,)), dma((2,)),
             ],
             compiler_params=pltpu.CompilerParams(vmem_limit_bytes=VMEM_LIMIT),
@@ -398,33 +393,31 @@
         )(positions, hidden, norm_attn[None, :], freq, w_qkv, k_cache.reshape(flat), v_cache.reshape(flat))
 
         units = w_down.shape[0]
-        n_chip = n_sp // 2
-        half_rows, group_rows, half = rows // 2, 2 * per_share, model // 2
+        chip_rows, half = 2 * per_share, model // 2
         result = pl.pallas_call(
             functools.partial(tail_kernel, n_tp, n_sp),
             out_shape=jax.ShapeDtypeStruct((rows, model), BF16),
             in_specs=[vmem(), hbm(), vmem(), hbm(), hbm(), hbm()],
             out_specs=vmem(),
             scratch_shapes=[
-                pltpu.VMEM(w_out.shape, BF16),
-                pltpu.VMEM((model, 2 * units // n_chip), BF16),
-                pltpu.VMEM((units, half), BF16),
-                pltpu.VMEM((per_share, model), F32),
+                pltpu.VMEM((w_out.shape[0], half), BF16),
+                pltpu.VMEM((model, units), BF16),
+                pltpu.VMEM((units // 2, half), BF16),
+                pltpu.VMEM((units // 2, half), BF16),
+                pltpu.VMEM((chip_rows, half), F32),
                 pltpu.VMEM((n_sp, per_share + 1, heads, head_dim), F32),
-                pltpu.VMEM((per_share * heads, head_dim), F32),
-                pltpu.VMEM((CHUNKS, n_tp, per_share, model // CHUNKS), F32),
-                pltpu.VMEM((CHUNKS, n_chip, per_share, model // CHUNKS), F32),
-                pltpu.VMEM((half_rows, model), F32),
-                pltpu.VMEM((half_rows, model), BF16),
-                pltpu.VMEM((half_rows // group_rows, group_rows, units // n_chip), F32),
-                pltpu.VMEM((n_chip, group_rows, units // n_chip), F32),
-                pltpu.VMEM((CHUNKS, n_tp, group_rows, half // CHUNKS), F32),
-                pltpu.VMEM((CHUNKS, n_sp, group_rows, half // CHUNKS), F32),
-                dma((7,)),
+                pltpu.VMEM((chip_rows * heads, head_dim), F32),
+                pltpu.VMEM((CHUNKS, n_tp, chip_rows, half // CHUNKS), F32),
+                pltpu.VMEM((2, CHUNKS, chip_rows, half // CHUNKS), F32),
+                pltpu.VMEM((chip_rows, model), BF16),
+                pltpu.VMEM((CHUNKS, chip_rows, half // CHUNKS), F32),
+                pltpu.VMEM((CHUNKS, chip_rows, half // CHUNKS), F32),
+                pltpu.VMEM((CHUNKS, n_tp, chip_rows, half // CHUNKS), F32),
+                pltpu.VMEM((CHUNKS, n_sp, chip_rows, half // CHUNKS), F32),
+                dma((4 + 2 * GU_SPLITS,)),
                 dma((n_sp - 1,)), dma((n_sp - 1,)),
+                dma((1 + 2 * CHUNKS,)), dma((1 + 2 * CHUNKS,)),
                 dma((CHUNKS, n_tp - 1)), dma((CHUNKS, n_tp - 1)),
-                dma((CHUNKS, n_chip - 1)), dma((CHUNKS, n_chip - 1)),
-                dma((2, n_chip - 1)), dma((2, n_chip - 1)),
                 dma((CHUNKS, n_tp - 1)), dma((CHUNKS, n_tp - 1)),
                 dma((CHUNKS, n_sp - 1)), dma((CHUNKS, n_sp - 1)),
             ],

time: 61.9 us -> 57.7 us (0.932)
  Pallas kernels: 59.4 us -> 55.2 us
    pallas_call x1, Pallas kernels: 41.7 us -> 39 us  [local_step(): pl.pallas_call(functools.partial(tail_kernel, n_tp, n_sp), out_shape=jax....]
    pallas_call x1, Pallas kernels: 17.8 us -> 16.2 us  [local_step(): pl.pallas_call(functools.partial(attend_kernel, (rows, block_len, kv_coun...]
where the time goes in v3:
time: 57.7 us; the launch traced here: 57.5 us
  Pallas kernels  55.2 us (96%)
  local copies, waits for them, and re-layouts  1.67 us (3%)
  between operations  0.65 us (1%)
    pallas_call x1, Pallas kernels, local_step(): pl.pallas_call(functools.partial(tail_kernel, n_tp, n_sp), out_shape=jax....  39 us
    pallas_call x1, Pallas kernels, local_step(): pl.pallas_call(functools.partial(attend_kernel, (rows, block_len, kv_coun...  16.2 us
    unnamed x1, local copies, waits for them, and re-layouts  1.67 us

profile of v3, /device:TPU:97, one launch (start us, length us, event | category | flops | bytes accessed | tf_op | source)
XLA Modules:
  0.0 57.5 jit_solution(5652592708185864269)
XLA Ops:
  0.6 16.2 %attend.1 = (bf16[32,1024,128]{2,1,0:T(8,128)(2,1)}, bf16[32,1024,128]{2,1,0:T(8,128)(2,1)}, f32[8,5,8,128]{3,2,1,0:T(8,128)}, f32[4,8,4096]{2,1,0:T(8,128)}) custom-call(s32[32]{0:T(128)} %pos_hbm.1, bf16[32,4096]{1,0:T(8,128)(2,1)} %hid_hbm.1, f32[1,4096]{1,0:T(1,128)} %bitcast.8, f32[1,128]{1,0:T(1,128)} %constant.2.clone.freq_hbm, ...), custom_call_target="tpu_custom_call" | custom-call | tf_op jit(solution)/shard_map/attend/pallas_call | solution.py:364
  16.8 39.0 %tail.1 = bf16[32,4096]{1,0:T(8,128)(2,1)} custom-call(f32[8,5,8,128]{3,2,1,0:T(8,128)} %get-tuple-element.7.part_ref, f32[4,8,4096]{2,1,0:T(8,128)} %get-tuple-element.8.resid_hbm, f32[1,4096]{1,0:T(1,128)} %bitcast.9, bf16[1024,4096]{1,0:T(8,128)(2,1)} %wo_hbm.1, bf16[4096,7168]{1,0:T(8,128)(2,1)} %wgu_hbm.1, bf16[3584,4096]{1,0:T(8,128)(2,1)} %wd_hbm.1), custom_call_target="tpu_custom_call" | custom-call | tf_op jit(solution)/shard_map/tail/pallas_call | solution.py:397
  55.9 1.7 %copy.15 = bf16[32,4096]{1,0:T(8,128)(2,1)} copy(bf16[32,4096]{1,0:T(8,128)(2,1)} %tail.1) | data formatting | bytes 524288

commit v4 on v3

--- a/solution.py
+++ b/solution.py
@@ -14,9 +14,11 @@
 MESH = pl.DeviceIdType.MESH
 LANES = 128
 QKV_CHUNKS = 4
-CHUNKS = 4
+OUT_CHUNKS = 2
+DOWN_CHUNKS = 2
 GU_SPLITS = 2
-VMEM_LIMIT = 60 * 1024 * 1024
+ATTEND_VMEM = 60 * 1024 * 1024
+TAIL_VMEM = 52 * 1024 * 1024
 F32, BF16 = jnp.float32, jnp.bfloat16
 
 
@@ -179,8 +181,8 @@
     part_copy.wait()
 
 
-def tail_kernel(n_tp, n_sp, part_ref, resid_hbm, gain_ref, wo_hbm, wgu_hbm, wd_hbm, out_ref,
-                wo_buf, wgu_buf, wd_own, wd_mate, resid_buf, part_in, att_buf, y1_buf, x1_in, r2_buf,
+def tail_kernel(n_tp, n_sp, part_hbm, resid_hbm, gain_hbm, wo_hbm, wgu_hbm, wd_hbm, out_ref,
+                gain_ref, wo_buf, wgu_buf, wd_own, wd_mate, resid_buf, part_in, att_buf, y1_buf, x1_own, r2_buf,
                 z_out, z_in, y2_buf, x2_in, w_sem, b_send, b_recv, m_send, m_recv, y1_send, y1_recv,
                 y2_send, y2_recv, g2_send, g2_recv):
     t = lax.axis_index('tp')
@@ -193,9 +195,10 @@
     core_units = units // 2
     split = core_units // GU_SPLITS
     half = model // 2
-    width = half // CHUNKS
-    per_share = part_ref.shape[1] - 1
-    heads = part_ref.shape[2]
+    width = half // OUT_CHUNKS
+    down_width = half // DOWN_CHUNKS
+    per_share = part_hbm.shape[1] - 1
+    heads = part_hbm.shape[2]
     share_rows = per_share * heads
     rows = 2 * per_share
 
@@ -215,8 +218,9 @@
         pltpu.make_async_copy(wd_hbm.at[wd_rows, columns(other, half)], wd_mate, w_sem.at[2]),
         pltpu.make_async_copy(wd_hbm.at[wd_rows, columns(core, half)], wd_own, w_sem.at[3]),
     ]
-    resid_load.start()
-    wo_load.start()
+    part_load = pltpu.make_async_copy(part_hbm.at[s], part_in.at[s], w_sem.at[4 + 2 * GU_SPLITS])
+    gain_load = pltpu.make_async_copy(gain_hbm, gain_ref, w_sem.at[5 + 2 * GU_SPLITS])
+    part_load.start()
 
     def wrap(value, count):
         return lax.rem(value + count, count)
@@ -226,6 +230,8 @@
         pl.semaphore_signal(barrier, inc=1, device_id={'sp': wrap(s + k, n_sp)}, device_id_type=MESH)
     for k in range(1, n_tp):
         pl.semaphore_signal(barrier, inc=1, device_id={'tp': wrap(t + k, n_tp)}, device_id_type=MESH)
+    resid_load.start()
+    gain_load.start()
     pl.semaphore_wait(barrier, n_sp + n_tp - 2)
 
     sent = []
@@ -244,9 +250,11 @@
 
     for k in range(1, n_sp):
         dev = wrap(s + k, n_sp)
-        push(part_ref.at[dev], part_in.at[s], b_send.at[k - 1], b_recv.at[k - 1], {'sp': dev})
-    part_in[s] = part_ref[s]
+        push(part_hbm.at[dev], part_in.at[s], b_send.at[k - 1], b_recv.at[k - 1], {'sp': dev})
+    wo_load.start()
+    part_load.wait()
     resid_load.wait()
+    gain_load.wait()
     wo_load.wait()
     for load in gu_loads[:2]:
         load.start()
@@ -267,30 +275,31 @@
     arrive(att_buf.at[pl.ds(pl.multiple_of(other * share_rows, heads), share_rows)], m_recv.at[0])
     attended = jnp.concatenate([att_buf[pl.ds(h, rows, stride=heads), :] for h in range(heads)], axis=1).astype(BF16)
 
-    for n in range(CHUNKS):
+    for n in range(OUT_CHUNKS):
         y1_buf[n, t] = round_bf16(dot(attended, wo_buf[:, n * width:(n + 1) * width]))
         for k in range(1, n_tp):
             push(y1_buf.at[n, t], y1_buf.at[n, t], y1_send.at[n, k - 1], y1_recv.at[n, k - 1], {'tp': wrap(t + k, n_tp)})
     for load in wd_loads:
         load.start()
-    for n in range(CHUNKS):
+    for n in range(OUT_CHUNKS):
         for k in range(1, n_tp):
             arrive(y1_buf.at[n, wrap(t - k, n_tp)], y1_recv.at[n, k - 1])
         out_sum = functools.reduce(jnp.add, [y1_buf[n, j] for j in range(n_tp)])
-        x1_in[core, n] = resid_buf[:, n * width:(n + 1) * width] + out_sum
-        push(x1_in.at[core, n], x1_in.at[core, n], m_send.at[1 + n], m_recv.at[1 + n], to_mate)
+        x1_own[core, :, n * width:(n + 1) * width] = resid_buf[:, n * width:(n + 1) * width] + out_sum
+        part = x1_own.at[core, :, pl.ds(n * width, width)]
+        push(part, part, m_send.at[1 + n], m_recv.at[1 + n], to_mate)
     square = jnp.zeros((rows, LANES), F32)
-    for n in range(CHUNKS):
-        arrive(x1_in.at[other, n], m_recv.at[1 + n])
+    for n in range(OUT_CHUNKS):
+        arrive(x1_own.at[other, :, pl.ds(n * width, width)], m_recv.at[1 + n])
         for c in range(2):
             for at in range(0, width, LANES):
-                piece = x1_in[c, n, :, at:at + LANES]
+                piece = x1_own[c, :, n * width + at:n * width + at + LANES]
                 square = square + piece * piece
     scale = lax.rsqrt(jnp.sum(square, axis=-1, keepdims=True) / model + NORM_EPS)
     for c in range(2):
-        for n in range(CHUNKS):
+        for n in range(OUT_CHUNKS):
             part = slice(c * half + n * width, c * half + (n + 1) * width)
-            r2_buf[:, part] = (x1_in[c, n] * scale * gain_ref[:, part]).astype(BF16)
+            r2_buf[:, part] = (x1_own[c, :, n * width:(n + 1) * width] * scale * gain_ref[:, part]).astype(BF16)
 
     acts = []
     for n in range(GU_SPLITS):
@@ -301,38 +310,38 @@
         acts.append((gate * jax.nn.sigmoid(gate) * both[:, split:]).astype(BF16))
     act = jnp.concatenate(acts, axis=1)
     wd_loads[0].wait()
-    for n in range(CHUNKS):
-        z_out[n] = dot(act, wd_mate[:, n * width:(n + 1) * width])
-        push(z_out.at[n], z_in.at[n], m_send.at[1 + CHUNKS + n], m_recv.at[1 + CHUNKS + n], to_mate)
+    for n in range(DOWN_CHUNKS):
+        z_out[n] = dot(act, wd_mate[:, n * down_width:(n + 1) * down_width])
+        push(z_out.at[n], z_in.at[n], m_send.at[1 + OUT_CHUNKS + n], m_recv.at[1 + OUT_CHUNKS + n], to_mate)
     wd_loads[1].wait()
-    for n in range(CHUNKS):
-        own = dot(act, wd_own[:, n * width:(n + 1) * width])
-        arrive(z_in.at[n], m_recv.at[1 + CHUNKS + n])
+    for n in range(DOWN_CHUNKS):
+        own = dot(act, wd_own[:, n * down_width:(n + 1) * down_width])
+        arrive(z_in.at[n], m_recv.at[1 + OUT_CHUNKS + n])
         y2_buf[n, t] = round_bf16(own + z_in[n])
         for k in range(1, n_tp):
             push(y2_buf.at[n, t], y2_buf.at[n, t], y2_send.at[n, k - 1], y2_recv.at[n, k - 1], {'tp': wrap(t + k, n_tp)})
-    for n in range(CHUNKS):
+    for n in range(DOWN_CHUNKS):
         for k in range(1, n_tp):
             arrive(y2_buf.at[n, wrap(t - k, n_tp)], y2_recv.at[n, k - 1])
         down_sum = functools.reduce(jnp.add, [y2_buf[n, j] for j in range(n_tp)])
-        x2_in[n, s] = x1_in[core, n] + down_sum
+        x2_in[n, s] = x1_own[core, :, n * down_width:(n + 1) * down_width] + down_sum
         for k in far_first:
             push(x2_in.at[n, s], x2_in.at[n, s], g2_send.at[n, k], g2_recv.at[n, k], {'sp': wrap(chip + k, n_chip) * 2 + core})
         push(x2_in.at[n, s], x2_in.at[n, s], g2_send.at[n, 0], g2_recv.at[n, 0], to_mate)
-    for n in range(CHUNKS):
+    for n in range(DOWN_CHUNKS):
         for k in near_first:
             far = x2_in.at[n, wrap(chip - k, n_chip) * 2 + core]
             arrive(far, g2_recv.at[n, k])
             push(far, far, g2_send.at[n, n_chip + k - 1], g2_recv.at[n, n_chip + k - 1], to_mate)
-    for n in range(CHUNKS):
+    for n in range(DOWN_CHUNKS):
         arrive(x2_in.at[n, mate], g2_recv.at[n, 0])
         for k in near_first:
             arrive(x2_in.at[n, wrap(chip - k, n_chip) * 2 + other], g2_recv.at[n, n_chip + k - 1])
         for j in range(0, n_chip, 2):
             for c in range(2):
                 lines = jnp.concatenate([x2_in[n, 2 * j + c], x2_in[n, 2 * j + 2 + c]], axis=0)
-                col = c * half + n * width
-                out_ref[j * rows:(j + 2) * rows, col:col + width] = lines.astype(BF16)
+                col = c * half + n * down_width
+                out_ref[j * rows:(j + 2) * rows, col:col + down_width] = lines.astype(BF16)
     for copy in sent:
         copy.wait_send()
 
@@ -366,8 +375,8 @@
             out_shape=(
                 jax.ShapeDtypeStruct(flat, BF16),
                 jax.ShapeDtypeStruct(flat, BF16),
-                jax.ShapeDtypeStruct((shares, per_share + 1, heads, head_dim), F32),
-                jax.ShapeDtypeStruct((shares // 2, 2 * per_share, model), F32),
+                pltpu.VMEM((shares, per_share + 1, heads, head_dim), F32),
+                pltpu.VMEM((shares // 2, 2 * per_share, model), F32),
             ),
             in_specs=[hbm()] * 7,
             out_specs=(hbm(), hbm(), hbm(), hbm()),
@@ -388,7 +397,7 @@
                 pltpu.VMEM((shares // 2, 2 * per_share, model), F32),
                 dma((4,)), dma((QKV_CHUNKS,)), dma((shares,)), dma((shares,)), dma((shares,)), dma((shares,)), dma((2,)),
             ],
-            compiler_params=pltpu.CompilerParams(vmem_limit_bytes=VMEM_LIMIT),
+            compiler_params=pltpu.CompilerParams(vmem_limit_bytes=ATTEND_VMEM),
             name='attend',
         )(positions, hidden, norm_attn[None, :], freq, w_qkv, k_cache.reshape(flat), v_cache.reshape(flat))
 
@@ -396,10 +405,11 @@
         chip_rows, half = 2 * per_share, model // 2
         result = pl.pallas_call(
             functools.partial(tail_kernel, n_tp, n_sp),
-            out_shape=jax.ShapeDtypeStruct((rows, model), BF16),
-            in_specs=[vmem(), hbm(), vmem(), hbm(), hbm(), hbm()],
+            out_shape=pltpu.VMEM((rows, model), BF16),
+            in_specs=[hbm()] * 6,
             out_specs=vmem(),
             scratch_shapes=[
+                pltpu.VMEM((1, model), F32),
                 pltpu.VMEM((w_out.shape[0], half), BF16),
                 pltpu.VMEM((model, units), BF16),
                 pltpu.VMEM((units // 2, half), BF16),
@@ -407,21 +417,21 @@
                 pltpu.VMEM((chip_rows, half), F32),
                 pltpu.VMEM((n_sp, per_share + 1, heads, head_dim), F32),
                 pltpu.VMEM((chip_rows * heads, head_dim), F32),
-                pltpu.VMEM((CHUNKS, n_tp, chip_rows, half // CHUNKS), F32),
-                pltpu.VMEM((2, CHUNKS, chip_rows, half // CHUNKS), F32),
+                pltpu.VMEM((OUT_CHUNKS, n_tp, chip_rows, half // OUT_CHUNKS), F32),
+                pltpu.VMEM((2, chip_rows, half), F32),
                 pltpu.VMEM((chip_rows, model), BF16),
-                pltpu.VMEM((CHUNKS, chip_rows, half // CHUNKS), F32),
-                pltpu.VMEM((CHUNKS, chip_rows, half // CHUNKS), F32),
-                pltpu.VMEM((CHUNKS, n_tp, chip_rows, half // CHUNKS), F32),
-                pltpu.VMEM((CHUNKS, n_sp, chip_rows, half // CHUNKS), F32),
-                dma((4 + 2 * GU_SPLITS,)),
+                pltpu.VMEM((DOWN_CHUNKS, chip_rows, half // DOWN_CHUNKS), F32),
+                pltpu.VMEM((DOWN_CHUNKS, chip_rows, half // DOWN_CHUNKS), F32),
+                pltpu.VMEM((DOWN_CHUNKS, n_tp, chip_rows, half // DOWN_CHUNKS), F32),
+                pltpu.VMEM((DOWN_CHUNKS, n_sp, chip_rows, half // DOWN_CHUNKS), F32),
+                dma((6 + 2 * GU_SPLITS,)),
                 dma((n_sp - 1,)), dma((n_sp - 1,)),
-                dma((1 + 2 * CHUNKS,)), dma((1 + 2 * CHUNKS,)),
-                dma((CHUNKS, n_tp - 1)), dma((CHUNKS, n_tp - 1)),
-                dma((CHUNKS, n_tp - 1)), dma((CHUNKS, n_tp - 1)),
-                dma((CHUNKS, n_sp - 1)), dma((CHUNKS, n_sp - 1)),
+                dma((1 + OUT_CHUNKS + DOWN_CHUNKS,)), dma((1 + OUT_CHUNKS + DOWN_CHUNKS,)),
+                dma((OUT_CHUNKS, n_tp - 1)), dma((OUT_CHUNKS, n_tp - 1)),
+                dma((DOWN_CHUNKS, n_tp - 1)), dma((DOWN_CHUNKS, n_tp - 1)),
+                dma((DOWN_CHUNKS, n_sp - 1)), dma((DOWN_CHUNKS, n_sp - 1)),
             ],
-            compiler_params=pltpu.CompilerParams(vmem_limit_bytes=VMEM_LIMIT, collective_id=0, has_side_effects=True),
+            compiler_params=pltpu.CompilerParams(vmem_limit_bytes=TAIL_VMEM, collective_id=0, has_side_effects=True),
             name='tail',
         )(parts, resid, norm_mlp[None, :], w_out, w_gate_up, w_down)
         return result, k_upd.reshape(k_cache.shape), v_upd.reshape(v_cache.shape)

time: 57.7 us -> 55.2 us (0.957)
  Pallas kernels: 55.2 us -> 53.8 us
  local copies, waits for them, and re-layouts: 1.67 us -> 0.71 us
    pallas_call x1, Pallas kernels: 39 us -> 37.8 us  [local_step(): pl.pallas_call(functools.partial(tail_kernel, n_tp, n_sp), out_shape=pltp...]
    unnamed x1 -> x3, local copies, waits for them, and re-layouts: 1.67 us -> 0.71 us
where the time goes in v4:
time: 55.2 us; the launch traced here: 55.1 us
  Pallas kernels  53.8 us (97%)
  local copies, waits for them, and re-layouts  0.71 us (1%)
  between operations  0.66 us (1%)
    pallas_call x1, Pallas kernels, local_step(): pl.pallas_call(functools.partial(tail_kernel, n_tp, n_sp), out_shape=pltp...  37.8 us
    pallas_call x1, Pallas kernels, local_step(): pl.pallas_call(functools.partial(attend_kernel, (rows, block_len, kv_coun...  16 us

profile of v4, /device:TPU:97, one launch (start us, length us, event | category | flops | bytes accessed | tf_op | source)
XLA Modules:
  0.0 55.1 jit_solution(176792241936263238)
XLA Ops:
  0.6 0.0 copy-start
  0.6 16.0 %attend.1 = (bf16[32,1024,128]{2,1,0:T(8,128)(2,1)}, bf16[32,1024,128]{2,1,0:T(8,128)(2,1)}, f32[8,5,8,128]{3,2,1,0:T(8,128)S(1)}, f32[4,8,4096]{2,1,0:T(8,128)S(1)}) custom-call(s32[32]{0:T(128)} %pos_hbm.1, bf16[32,4096]{1,0:T(8,128)(2,1)} %hid_hbm.1, f32[1,4096]{1,0:T(1,128)} %bitcast.9, f32[1,128]{1,0:T(1,128)} %constant.2.clone.freq_hbm, ...), custom_call_target="tpu_custom_call" | custom-call | tf_op jit(solution)/shard_map/attend/pallas_call | solution.py:373
  16.7 0.0 copy-done
  16.7 37.8 %tail.1 = bf16[32,4096]{1,0:T(8,128)(2,1)S(1)} custom-call(f32[8,5,8,128]{3,2,1,0:T(8,128)S(1)} %get-tuple-element.7.part_hbm, f32[4,8,4096]{2,1,0:T(8,128)S(1)} %get-tuple-element.8.resid_hbm, f32[1,4096]{1,0:T(1,128)S(1)} %bitcast.6, bf16[1024,4096]{1,0:T(8,128)(2,1)} %wo_hbm.1, bf16[4096,7168]{1,0:T(8,128)(2,1)} %wgu_hbm.1, bf16[3584,4096]{1,0:T(8,128)(2,1)} %wd_hbm.1), custom_call_target="tpu_custom_call" | custom-call | tf_op jit(solution)/shard_map/tail/pallas_call | solution.py:406
  54.4 0.7 %copy.15 = bf16[32,4096]{1,0:T(8,128)(2,1)} copy(bf16[32,4096]{1,0:T(8,128)(2,1)S(1)} %tail.1) | data formatting | bytes 524288
Async XLA Ops:
  0.6 16.0 %copy-start = (f32[4096]{0:T(1024)S(1)}, f32[4096]{0:T(1024)}, u32[]{:S(2)}) copy-start(f32[4096]{0:T(1024)} %param.14) | copy-start | bytes 49156

commit v5 on v4

--- a/solution.py
+++ b/solution.py
@@ -16,7 +16,7 @@
 QKV_CHUNKS = 4
 OUT_CHUNKS = 2
 DOWN_CHUNKS = 2
-GU_SPLITS = 2
+GU_SPLITS = 1
 ATTEND_VMEM = 60 * 1024 * 1024
 TAIL_VMEM = 52 * 1024 * 1024
 F32, BF16 = jnp.float32, jnp.bfloat16
@@ -248,18 +248,21 @@
     near_first = sorted(range(1, n_chip), key=lambda k: min(k, n_chip - k))
     far_first = near_first[::-1]
 
-    for k in range(1, n_sp):
-        dev = wrap(s + k, n_sp)
-        push(part_hbm.at[dev], part_in.at[s], b_send.at[k - 1], b_recv.at[k - 1], {'sp': dev})
+    links = [(k, c) for k in far_first + [0] for c in range(2) if k or c]
+    for n, (k, c) in enumerate(links):
+        dev = wrap(chip + k, n_chip) * 2 + lax.rem(core + c, 2)
+        push(part_hbm.at[dev], part_in.at[s], b_send.at[n], b_recv.at[n], {'sp': dev})
     wo_load.start()
+    for load in gu_loads[:2]:
+        load.start()
     part_load.wait()
     resid_load.wait()
     gain_load.wait()
     wo_load.wait()
-    for load in gu_loads[:2]:
+    for n, (k, c) in enumerate(links):
+        arrive(part_in.at[wrap(chip - k, n_chip) * 2 + lax.rem(core + c, 2)], b_recv.at[n])
+    for load in gu_loads[2:]:
         load.start()
-    for k in range(1, n_sp):
-        arrive(part_in.at[wrap(s - k, n_sp)], b_recv.at[k - 1])
     stats = [part_in[j, per_share] for j in range(n_sp)]
     top = functools.reduce(jnp.maximum, stats)
     scales = [jnp.exp(st - top) for st in stats]
@@ -270,17 +273,15 @@
         att_buf[pl.ds(at, heads), :] = round_bf16(acc / total[:, i:i + 1])
     mine = att_buf.at[pl.ds(pl.multiple_of(core * share_rows, heads), share_rows)]
     push(mine, mine, m_send.at[0], m_recv.at[0], to_mate)
-    for load in gu_loads[2:]:
-        load.start()
     arrive(att_buf.at[pl.ds(pl.multiple_of(other * share_rows, heads), share_rows)], m_recv.at[0])
     attended = jnp.concatenate([att_buf[pl.ds(h, rows, stride=heads), :] for h in range(heads)], axis=1).astype(BF16)
 
+    for load in wd_loads:
+        load.start()
     for n in range(OUT_CHUNKS):
         y1_buf[n, t] = round_bf16(dot(attended, wo_buf[:, n * width:(n + 1) * width]))
-        for k in range(1, n_tp):
+        for k in sorted(range(1, n_tp), key=lambda k: -min(k, n_tp - k)):
             push(y1_buf.at[n, t], y1_buf.at[n, t], y1_send.at[n, k - 1], y1_recv.at[n, k - 1], {'tp': wrap(t + k, n_tp)})
-    for load in wd_loads:
-        load.start()
     for n in range(OUT_CHUNKS):
         for k in range(1, n_tp):
             arrive(y1_buf.at[n, wrap(t - k, n_tp)], y1_recv.at[n, k - 1])
@@ -310,15 +311,16 @@
         acts.append((gate * jax.nn.sigmoid(gate) * both[:, split:]).astype(BF16))
     act = jnp.concatenate(acts, axis=1)
     wd_loads[0].wait()
+    given = dot(act, wd_mate[...])
     for n in range(DOWN_CHUNKS):
-        z_out[n] = dot(act, wd_mate[:, n * down_width:(n + 1) * down_width])
+        z_out[n] = given[:, n * down_width:(n + 1) * down_width]
         push(z_out.at[n], z_in.at[n], m_send.at[1 + OUT_CHUNKS + n], m_recv.at[1 + OUT_CHUNKS + n], to_mate)
     wd_loads[1].wait()
     for n in range(DOWN_CHUNKS):
         own = dot(act, wd_own[:, n * down_width:(n + 1) * down_width])
         arrive(z_in.at[n], m_recv.at[1 + OUT_CHUNKS + n])
         y2_buf[n, t] = round_bf16(own + z_in[n])
-        for k in range(1, n_tp):
+        for k in sorted(range(1, n_tp), key=lambda k: -min(k, n_tp - k)):
             push(y2_buf.at[n, t], y2_buf.at[n, t], y2_send.at[n, k - 1], y2_recv.at[n, k - 1], {'tp': wrap(t + k, n_tp)})
     for n in range(DOWN_CHUNKS):
         for k in range(1, n_tp):

time: 55.2 us -> 54 us (0.978)
  Pallas kernels: 53.8 us -> 52.6 us
    pallas_call x1, Pallas kernels: 37.8 us -> 36.6 us  [local_step(): pl.pallas_call(functools.partial(tail_kernel, n_tp, n_sp), out_shape=pltp...]
where the time goes in v5:
time: 54 us
  Pallas kernels  52.6 us (97%)
  local copies, waits for them, and re-layouts  0.71 us (1%)
  between operations  0.66 us (1%)
    pallas_call x1, Pallas kernels, local_step(): pl.pallas_call(functools.partial(tail_kernel, n_tp, n_sp), out_shape=pltp...  36.6 us
    pallas_call x1, Pallas kernels, local_step(): pl.pallas_call(functools.partial(attend_kernel, (rows, block_len, kv_coun...  16 us

profile of v5, /device:TPU:97, one launch (start us, length us, event | category | flops | bytes accessed | tf_op | source)
XLA Modules:
  0.0 54.0 jit_solution(15209070727904034353)
XLA Ops:
  0.6 0.0 copy-start
  0.6 16.0 %attend.1 = (bf16[32,1024,128]{2,1,0:T(8,128)(2,1)}, bf16[32,1024,128]{2,1,0:T(8,128)(2,1)}, f32[8,5,8,128]{3,2,1,0:T(8,128)S(1)}, f32[4,8,4096]{2,1,0:T(8,128)S(1)}) custom-call(s32[32]{0:T(128)} %pos_hbm.1, bf16[32,4096]{1,0:T(8,128)(2,1)} %hid_hbm.1, f32[1,4096]{1,0:T(1,128)} %bitcast.9, f32[1,128]{1,0:T(1,128)} %constant.2.clone.freq_hbm, ...), custom_call_target="tpu_custom_call" | custom-call | tf_op jit(solution)/shard_map/attend/pallas_call | solution.py:375
  16.7 0.0 copy-done
  16.7 36.6 %tail.1 = bf16[32,4096]{1,0:T(8,128)(2,1)S(1)} custom-call(f32[8,5,8,128]{3,2,1,0:T(8,128)S(1)} %get-tuple-element.7.part_hbm, f32[4,8,4096]{2,1,0:T(8,128)S(1)} %get-tuple-element.8.resid_hbm, f32[1,4096]{1,0:T(1,128)S(1)} %bitcast.6, bf16[1024,4096]{1,0:T(8,128)(2,1)} %wo_hbm.1, bf16[4096,7168]{1,0:T(8,128)(2,1)} %wgu_hbm.1, bf16[3584,4096]{1,0:T(8,128)(2,1)} %wd_hbm.1), custom_call_target="tpu_custom_call" | custom-call | tf_op jit(solution)/shard_map/tail/pallas_call | solution.py:408
  53.3 0.7 %copy.15 = bf16[32,4096]{1,0:T(8,128)(2,1)} copy(bf16[32,4096]{1,0:T(8,128)(2,1)S(1)} %tail.1) | data formatting | bytes 524288
Async XLA Ops:
  0.6 16.0 %copy-start = (f32[4096]{0:T(1024)S(1)}, f32[4096]{0:T(1024)}, u32[]{:S(2)}) copy-start(f32[4096]{0:T(1024)} %param.14) | copy-start | bytes 49156
